TPU v7x, 1024 devices: a whole 4x8x16 slice. The times are simulated.
1024 devices in a mesh: gx: 16 (over z), gy: 8 (over x, core), gz: 8 (over y).
Axes of the slice: x: 4, y: 8, z: 16, core: 2. Of those that a mesh axis runs over, the one named last changes fastest.
Arguments:
- dist: float32 [19, 32, 64, 2048], P(None, 'gx', 'gy', 'gz'), may hold values from 0.01 to 0.1
- site_kinds: int32 [32, 64, 2048], P('gx', 'gy', 'gz'), may hold values from 0 to 3
- relax: float32 [32, 64, 2048], P('gx', 'gy', 'gz'), may hold values from 0.5 to 1.9
- inflow: float32 [3, 32, 64, 2048], P(None, 'gx', 'gy', 'gz'), may hold values from -0.3 to 0.3
Outputs:
- density: float32 [32, 64, 2048], P('gx', 'gy', 'gz')
- momentum: float32 [3, 32, 64, 2048], P(None, 'gx', 'gy', 'gz')
All inputs are finite; a program needn't handle non-finite values.
Results may differ from a plain program's by a relative error of at most 0.0001.
Values sent between devices are 32-bit elements; how exact they have to be, the bound alone decides.
A program may use at most 32 MiB of HBM per device.

v0:
```python
import jax
import jax.numpy as jnp
import numpy as np
from jax import lax
from jax.sharding import PartitionSpec as P

STEPS = 2


VELOCITIES = [
    (0, 0, 0),
    (1, 0, 0),
    (-1, 0, 0),
    (0, 1, 0),
    (0, -1, 0),
    (0, 0, 1),
    (0, 0, -1),
    (1, 1, 0),
    (-1, -1, 0),
    (1, -1, 0),
    (-1, 1, 0),
    (1, 0, 1),
    (-1, 0, -1),
    (1, 0, -1),
    (-1, 0, 1),
    (0, 1, 1),
    (0, -1, -1),
    (0, 1, -1),
    (0, -1, 1),
]
WEIGHTS = [1.0 / 3.0] + [1.0 / 18.0] * 6 + [1.0 / 36.0] * 12
OPPOSITE = [0, 2, 1, 4, 3, 6, 5, 8, 7, 10, 9, 12, 11, 14, 13, 16, 15, 18, 17]


def passed_along(block, axis, distance):
    devices = range(lax.axis_size(axis))
    route = [(i - distance, i) for i in devices if i - distance in devices]
    return lax.ppermute(block, axis, route)


def moments(dist):
    table = np.array(VELOCITIES, dtype=np.float32)
    density = jnp.sum(dist, axis=0)
    parts = []
    for axis_id in range(3):
        column = jnp.asarray(table[:, axis_id]).astype(dist.dtype)
        parts.append(jnp.sum(column[:, None, None, None] * dist, axis=0))
    return (density, jnp.stack(parts))


def equilibrium(density, speed):
    usq = speed[0] * speed[0] + speed[1] * speed[1] + speed[2] * speed[2]
    result = []
    for index in range(19):
        vel = VELOCITIES[index]
        along = vel[0] * speed[0] + vel[1] * speed[1] + vel[2] * speed[2]
        result.append(WEIGHTS[index] * (density + 3.0 * along + 4.5 * along * along - 1.5 * usq))
    return jnp.stack(result)


def collide(dist, site_kinds, relax, inflow):
    density, speed = moments(dist)
    fluid = dist - relax[None] * (dist - equilibrium(density, speed))
    wall = dist[np.array(OPPOSITE)]
    inlet = equilibrium(density, inflow)
    outlet = equilibrium(jnp.ones_like(density), speed)
    kinds = site_kinds[None]
    return jnp.where(
        kinds == 0, wall, jnp.where(kinds == 1, fluid, jnp.where(kinds == 2, inlet, outlet))
    )


def chosen(axis_id, sign):
    return [index for index in range(19) if VELOCITIES[index][axis_id] == sign]


def forward(stack, edge, dim):
    inner = lax.slice_in_dim(stack, 0, stack.shape[dim] - 1, axis=dim)
    return jnp.concatenate([jnp.expand_dims(edge, dim), inner], axis=dim)


def backward(stack, edge, dim):
    inner = lax.slice_in_dim(stack, 1, stack.shape[dim], axis=dim)
    return jnp.concatenate([inner, jnp.expand_dims(edge, dim)], axis=dim)


def last_plane(stack, dim):
    return lax.index_in_dim(stack, stack.shape[dim] - 1, axis=dim, keepdims=False)


def first_plane(stack, dim):
    return lax.index_in_dim(stack, 0, axis=dim, keepdims=False)


def shards(dist, site_kinds, relax, inflow):
    field = dist
    for step in range(STEPS):
        post = collide(field, site_kinds, relax, inflow)
        pops = [post[index] for index in range(19)]
        upper = chosen(0, 1)
        lower = chosen(0, -1)
        stack_up = jnp.stack([pops[index] for index in upper])
        stack_down = jnp.stack([pops[index] for index in lower])
        edge_up = passed_along(last_plane(stack_up, 1), "gx", 1)
        edge_down = passed_along(first_plane(stack_down, 1), "gx", -1)
        stack_up = forward(stack_up, edge_up, 1)
        stack_down = backward(stack_down, edge_down, 1)
        for slot, index in enumerate(upper):
            pops[index] = stack_up[slot]
        for slot, index in enumerate(lower):
            pops[index] = stack_down[slot]
        upper = chosen(1, 1)
        lower = chosen(1, -1)
        stack_up = jnp.stack([pops[index] for index in upper])
        stack_down = jnp.stack([pops[index] for index in lower])
        edge_up = passed_along(last_plane(stack_up, 2), "gy", 1)
        edge_down = passed_along(first_plane(stack_down, 2), "gy", -1)
        stack_up = forward(stack_up, edge_up, 2)
        stack_down = backward(stack_down, edge_down, 2)
        for slot, index in enumerate(upper):
            pops[index] = stack_up[slot]
        for slot, index in enumerate(lower):
            pops[index] = stack_down[slot]
        upper = chosen(2, 1)
        lower = chosen(2, -1)
        stack_up = jnp.stack([pops[index] for index in upper])
        stack_down = jnp.stack([pops[index] for index in lower])
        edge_up = passed_along(last_plane(stack_up, 3), "gz", 1)
        edge_down = passed_along(first_plane(stack_down, 3), "gz", -1)
        stack_up = forward(stack_up, edge_up, 3)
        stack_down = backward(stack_down, edge_down, 3)
        for slot, index in enumerate(upper):
            pops[index] = stack_up[slot]
        for slot, index in enumerate(lower):
            pops[index] = stack_down[slot]
        field = jnp.stack(pops)
    return moments(field)


def solution(mesh):
    return jax.shard_map(
        shards,
        mesh=mesh,
        in_specs=(
            P(None, "gx", "gy", "gz"),
            P("gx", "gy", "gz"),
            P("gx", "gy", "gz"),
            P(None, "gx", "gy", "gz"),
        ),
        out_specs=(P("gx", "gy", "gz"), P(None, "gx", "gy", "gz")),
        check_vma=False,
    )
```

profile of v0, /device:TPU:346, one launch (start us, length us, event | category | flops | bytes accessed | tf_op | source)
XLA Modules:
  0.0 69.5 jit_solution(14390502713386217045)
XLA Ops:
  1.3 1.1 %multiply_reduce_fusion.8 = (f32[2,8,256]{2,1,0:T(8,128)S(1)}, f32[2,8,256]{2,1,0:T(8,128)S(1)}, f32[2,8,256]{2,1,0:T(8,128)S(1)}, f32[2,8,256]{2,1,0:T(8,128)S(1)}) fusion(f32[19,2,8,256]{3,2,1,0:T(8,128)} %param.17, f32[19]{0:T(128)S(1)} %copy-done.4, f32[19]{0:T(128)S(1)} %copy-done.5, f32[19]{0:T(128)S(1)} %copy-done.6), kind=kLoop, calls=%fused_computation.216 | loop fusion | flops 528384 | bytes 377060 | tf_op jit(solution)/shard_map/reduce_sum | solution.py:47
  2.9 0.8 %copy-done = f32[3,2,8,256]{3,2,1,0:T(8,128)S(1)} copy-done((f32[3,2,8,256]{3,2,1,0:T(8,128)S(1)}, f32[3,2,8,256]{3,2,1,0:T(8,128)}, u32[]{:S(2)}) %copy-start) | copy-done | bytes 49176
  4.1 0.7 copy-done.3
  4.8 0.6 copy-done.7
  6.5 4.3 %collective-permute-start = (f32[5,8,256]{2,1,0:T(8,128)S(1)}, f32[5,8,256]{2,1,0:T(8,128)S(1)}, u32[]{:S(2)}, u32[]{:S(2)}) collective-permute-start(f32[5,8,256]{2,1,0:T(8,128)S(1)} %get-tuple-element.132), channel_id=1, source_target_pairs={{0,64},{64,128},{128,192},{192,256},{256,320},{320,384},{384,448},... | collective-permute-start | bytes 122888 | tf_op jit(solution)/shard_map/ppermute | solution.py:38
  10.8 1.9 %collective-permute-start.1 = (f32[5,8,256]{2,1,0:T(8,128)S(1)}, f32[5,8,256]{2,1,0:T(8,128)S(1)}, u32[]{:S(2)}, u32[]{:S(2)}) collective-permute-start(f32[5,8,256]{2,1,0:T(8,128)S(1)} %get-tuple-element.131), channel_id=1, source_target_pairs={{64,0},{128,64},{192,128},{256,192},{320,256},{384,320},{448,384},... | collective-permute-start | bytes 122888 | tf_op jit(solution)/shard_map/ppermute | solution.py:38
  12.8 4.3 %collective-permute-done.1 = f32[5,8,256]{2,1,0:T(8,128)S(1)} collective-permute-done((f32[5,8,256]{2,1,0:T(8,128)S(1)}, f32[5,8,256]{2,1,0:T(8,128)S(1)}, u32[]{:S(2)}, u32[]{:S(2)}) %collective-permute-start.1) | collective-permute-done | bytes 40992 | tf_op jit(solution)/shard_map/ppermute | solution.py:38
  17.2 1.9 %collective-permute-start.3 = (f32[5,2,256]{2,1,0:T(2,128)S(1)}, f32[5,2,256]{2,1,0:T(2,128)S(1)}, u32[]{:S(2)}, u32[]{:S(2)}) collective-permute-start(f32[5,2,256]{2,1,0:T(2,128)S(1)} %bitcast.931), channel_id=1, source_target_pairs={{8,0},{16,8},{24,16},{32,24},{40,32},{48,40},{56,48},{9,1},{17,9},... | collective-permute-start | bytes 30728 | tf_op jit(solution)/shard_map/ppermute | solution.py:38
  19.1 2.4 %collective-permute-start.2 = (f32[5,2,256]{2,1,0:T(2,128)S(1)}, f32[5,2,256]{2,1,0:T(2,128)S(1)}, u32[]{:S(2)}, u32[]{:S(2)}) collective-permute-start(f32[5,2,256]{2,1,0:T(2,128)S(1)} %bitcast.935), channel_id=1, source_target_pairs={{0,8},{8,16},{16,24},{24,32},{32,40},{40,48},{48,56},{1,9},{9,17},... | collective-permute-start | bytes 30728 | tf_op jit(solution)/shard_map/ppermute | solution.py:38
  21.6 2.5 %collective-permute-done.2 = f32[5,2,256]{2,1,0:T(2,128)S(1)} collective-permute-done((f32[5,2,256]{2,1,0:T(2,128)S(1)}, f32[5,2,256]{2,1,0:T(2,128)S(1)}, u32[]{:S(2)}, u32[]{:S(2)}) %collective-permute-start.2) | collective-permute-done | bytes 10272 | tf_op jit(solution)/shard_map/ppermute | solution.py:38
  24.3 2.4 %collective-permute-start.5 = (f32[5,2,8]{2,1,0:T(2,128)S(1)}, f32[5,2,8]{2,1,0:T(2,128)S(1)}, u32[]{:S(2)}, u32[]{:S(2)}) collective-permute-start(f32[5,2,8]{2,1,0:T(2,128)S(1)} %slice_reduce_fusion.2), channel_id=1, source_target_pairs={{1,0},{2,1},{3,2},{4,3},{5,4},{6,5},{7,6},{9,8},{10,9},{11,10},{12... | collective-permute-start | bytes 968 | tf_op jit(solution)/shard_map/ppermute | solution.py:38
  26.8 4.7 %collective-permute-start.4 = (f32[5,2,8]{2,1,0:T(2,128)S(1)}, f32[5,2,8]{2,1,0:T(2,128)S(1)}, u32[]{:S(2)}, u32[]{:S(2)}) collective-permute-start(f32[5,2,8]{2,1,0:T(2,128)S(1)} %slice_reduce_fusion.3), channel_id=1, source_target_pairs={{0,1},{1,2},{2,3},{3,4},{4,5},{5,6},{6,7},{8,9},{9,10},{10,11},{11... | collective-permute-start | bytes 968 | tf_op jit(solution)/shard_map/ppermute | solution.py:38
  31.8 1.1 %collective-permute-done.4 = f32[5,2,8]{2,1,0:T(2,128)S(1)} collective-permute-done((f32[5,2,8]{2,1,0:T(2,128)S(1)}, f32[5,2,8]{2,1,0:T(2,128)S(1)}, u32[]{:S(2)}, u32[]{:S(2)}) %collective-permute-start.4) | collective-permute-done | bytes 352 | tf_op jit(solution)/shard_map/ppermute | solution.py:38
  35.2 5.5 %collective-permute-start.6 = (f32[5,8,256]{2,1,0:T(8,128)S(1)}, f32[5,8,256]{2,1,0:T(8,128)S(1)}, u32[]{:S(2)}, u32[]{:S(2)}) collective-permute-start(f32[5,8,256]{2,1,0:T(8,128)S(1)} %get-tuple-element.120), channel_id=1, source_target_pairs={{0,64},{64,128},{128,192},{192,256},{256,320},{320,384},{384,448},... | collective-permute-start | bytes 122888 | tf_op jit(solution)/shard_map/ppermute | solution.py:38
  40.7 1.9 %collective-permute-start.7 = (f32[5,8,256]{2,1,0:T(8,128)S(1)}, f32[5,8,256]{2,1,0:T(8,128)S(1)}, u32[]{:S(2)}, u32[]{:S(2)}) collective-permute-start(f32[5,8,256]{2,1,0:T(8,128)S(1)} %get-tuple-element.119), channel_id=1, source_target_pairs={{64,0},{128,64},{192,128},{256,192},{320,256},{384,320},{448,384},... | collective-permute-start | bytes 122888 | tf_op jit(solution)/shard_map/ppermute | solution.py:38
  42.7 5.2 %collective-permute-done.7 = f32[5,8,256]{2,1,0:T(8,128)S(1)} collective-permute-done((f32[5,8,256]{2,1,0:T(8,128)S(1)}, f32[5,8,256]{2,1,0:T(8,128)S(1)}, u32[]{:S(2)}, u32[]{:S(2)}) %collective-permute-start.7) | collective-permute-done | bytes 40992 | tf_op jit(solution)/shard_map/ppermute | solution.py:38
  47.9 1.9 %collective-permute-start.9 = (f32[5,2,256]{2,1,0:T(2,128)S(1)}, f32[5,2,256]{2,1,0:T(2,128)S(1)}, u32[]{:S(2)}, u32[]{:S(2)}) collective-permute-start(f32[5,2,256]{2,1,0:T(2,128)S(1)} %bitcast.933), channel_id=1, source_target_pairs={{8,0},{16,8},{24,16},{32,24},{40,32},{48,40},{56,48},{9,1},{17,9},... | collective-permute-start | bytes 30728 | tf_op jit(solution)/shard_map/ppermute | solution.py:38
  49.9 2.4 %collective-permute-start.8 = (f32[5,2,256]{2,1,0:T(2,128)S(1)}, f32[5,2,256]{2,1,0:T(2,128)S(1)}, u32[]{:S(2)}, u32[]{:S(2)}) collective-permute-start(f32[5,2,256]{2,1,0:T(2,128)S(1)} %bitcast.937), channel_id=1, source_target_pairs={{0,8},{8,16},{16,24},{24,32},{32,40},{40,48},{48,56},{1,9},{9,17},... | collective-permute-start | bytes 30728 | tf_op jit(solution)/shard_map/ppermute | solution.py:38
  52.3 2.5 %collective-permute-done.8 = f32[5,2,256]{2,1,0:T(2,128)S(1)} collective-permute-done((f32[5,2,256]{2,1,0:T(2,128)S(1)}, f32[5,2,256]{2,1,0:T(2,128)S(1)}, u32[]{:S(2)}, u32[]{:S(2)}) %collective-permute-start.8) | collective-permute-done | bytes 10272 | tf_op jit(solution)/shard_map/ppermute | solution.py:38
  55.1 5.4 %collective-permute-start.10 = (f32[5,2,8]{2,1,0:T(2,128)S(1)}, f32[5,2,8]{2,1,0:T(2,128)S(1)}, u32[]{:S(2)}, u32[]{:S(2)}) collective-permute-start(f32[5,2,8]{2,1,0:T(2,128)S(1)} %slice_reduce_fusion.1), channel_id=1, source_target_pairs={{0,1},{1,2},{2,3},{3,4},{4,5},{5,6},{6,7},{8,9},{9,10},{10,11},{11... | collective-permute-start | bytes 968 | tf_op jit(solution)/shard_map/ppermute | solution.py:38
  60.6 1.9 %collective-permute-start.11 = (f32[5,2,8]{2,1,0:T(2,128)S(1)}, f32[5,2,8]{2,1,0:T(2,128)S(1)}, u32[]{:S(2)}, u32[]{:S(2)}) collective-permute-start(f32[5,2,8]{2,1,0:T(2,128)S(1)} %slice_reduce_fusion), channel_id=1, source_target_pairs={{1,0},{2,1},{3,2},{4,3},{5,4},{6,5},{7,6},{9,8},{10,9},{11,10},{12... | collective-permute-start | bytes 968 | tf_op jit(solution)/shard_map/ppermute | solution.py:38
  62.8 4.6 %collective-permute-done.11 = f32[5,2,8]{2,1,0:T(2,128)S(1)} collective-permute-done((f32[5,2,8]{2,1,0:T(2,128)S(1)}, f32[5,2,8]{2,1,0:T(2,128)S(1)}, u32[]{:S(2)}, u32[]{:S(2)}) %collective-permute-start.11) | collective-permute-done | bytes 352 | tf_op jit(solution)/shard_map/ppermute | solution.py:38
  68.2 0.6 pad_maximum_fusion
  68.9 0.6 bitcast_add_fusion
  (186 shorter events, 6.4 us)
Async XLA Ops:
  0.6 0.7 copy-start.4
  0.6 0.7 copy-start.5
  0.7 0.7 copy-start.6
  2.9 0.8 %copy-start = (f32[3,2,8,256]{3,2,1,0:T(8,128)S(1)}, f32[3,2,8,256]{3,2,1,0:T(8,128)}, u32[]{:S(2)}) copy-start(f32[3,2,8,256]{3,2,1,0:T(8,128)} %param.20) | copy-start | bytes 147460
  4.0 1.5 %copy-start.1 = (f32[19,2,8,256]{3,2,1,0:T(8,128)S(1)}, f32[19,2,8,256]{3,2,1,0:T(8,128)}, u32[]{:S(2)}) copy-start(f32[19,2,8,256]{3,2,1,0:T(8,128)} %param.17) | copy-start | bytes 933892
  4.1 0.7 %copy-start.3 = (s32[2,8,256]{2,1,0:T(8,128)S(1)}, s32[2,8,256]{2,1,0:T(8,128)}, u32[]{:S(2)}) copy-start(s32[2,8,256]{2,1,0:T(8,128)} %param.18) | copy-start | bytes 49156
  4.8 0.7 copy-start.7
  5.5 0.7 %copy-start.2 = (f32[2,8,256]{2,1,0:T(8,128)S(1)}, f32[2,8,256]{2,1,0:T(8,128)}, u32[]{:S(2)}) copy-start(f32[2,8,256]{2,1,0:T(8,128)} %param.19) | copy-start | bytes 49156
  6.5 6.3 %collective-permute-start = (f32[5,8,256]{2,1,0:T(8,128)S(1)}, f32[5,8,256]{2,1,0:T(8,128)S(1)}, u32[]{:S(2)}, u32[]{:S(2)}) collective-permute-start(f32[5,8,256]{2,1,0:T(8,128)S(1)} %get-tuple-element.132), channel_id=1, source_target_pairs={{0,64},{64,128},{128,192},{192,256},{256,320},{320,384},{384,448},... | collective-permute-start | bytes 122888 | tf_op jit(solution)/shard_map/ppermute | solution.py:38
  10.8 6.3 %collective-permute-start.1 = (f32[5,8,256]{2,1,0:T(8,128)S(1)}, f32[5,8,256]{2,1,0:T(8,128)S(1)}, u32[]{:S(2)}, u32[]{:S(2)}) collective-permute-start(f32[5,8,256]{2,1,0:T(8,128)S(1)} %get-tuple-element.131), channel_id=1, source_target_pairs={{64,0},{128,64},{192,128},{256,192},{320,256},{384,320},{448,384},... | collective-permute-start | bytes 122888 | tf_op jit(solution)/shard_map/ppermute | solution.py:38
  17.2 4.4 %collective-permute-start.3 = (f32[5,2,256]{2,1,0:T(2,128)S(1)}, f32[5,2,256]{2,1,0:T(2,128)S(1)}, u32[]{:S(2)}, u32[]{:S(2)}) collective-permute-start(f32[5,2,256]{2,1,0:T(2,128)S(1)} %bitcast.931), channel_id=1, source_target_pairs={{8,0},{16,8},{24,16},{32,24},{40,32},{48,40},{56,48},{9,1},{17,9},... | collective-permute-start | bytes 30728 | tf_op jit(solution)/shard_map/ppermute | solution.py:38
  19.1 5.0 %collective-permute-start.2 = (f32[5,2,256]{2,1,0:T(2,128)S(1)}, f32[5,2,256]{2,1,0:T(2,128)S(1)}, u32[]{:S(2)}, u32[]{:S(2)}) collective-permute-start(f32[5,2,256]{2,1,0:T(2,128)S(1)} %bitcast.935), channel_id=1, source_target_pairs={{0,8},{8,16},{16,24},{24,32},{32,40},{40,48},{48,56},{1,9},{9,17},... | collective-permute-start | bytes 30728 | tf_op jit(solution)/shard_map/ppermute | solution.py:38
  24.3 7.3 %collective-permute-start.5 = (f32[5,2,8]{2,1,0:T(2,128)S(1)}, f32[5,2,8]{2,1,0:T(2,128)S(1)}, u32[]{:S(2)}, u32[]{:S(2)}) collective-permute-start(f32[5,2,8]{2,1,0:T(2,128)S(1)} %slice_reduce_fusion.2), channel_id=1, source_target_pairs={{1,0},{2,1},{3,2},{4,3},{5,4},{6,5},{7,6},{9,8},{10,9},{11,10},{12... | collective-permute-start | bytes 968 | tf_op jit(solution)/shard_map/ppermute | solution.py:38
  26.8 6.0 %collective-permute-start.4 = (f32[5,2,8]{2,1,0:T(2,128)S(1)}, f32[5,2,8]{2,1,0:T(2,128)S(1)}, u32[]{:S(2)}, u32[]{:S(2)}) collective-permute-start(f32[5,2,8]{2,1,0:T(2,128)S(1)} %slice_reduce_fusion.3), channel_id=1, source_target_pairs={{0,1},{1,2},{2,3},{3,4},{4,5},{5,6},{6,7},{8,9},{9,10},{10,11},{11... | collective-permute-start | bytes 968 | tf_op jit(solution)/shard_map/ppermute | solution.py:38
  35.2 7.4 %collective-permute-start.6 = (f32[5,8,256]{2,1,0:T(8,128)S(1)}, f32[5,8,256]{2,1,0:T(8,128)S(1)}, u32[]{:S(2)}, u32[]{:S(2)}) collective-permute-start(f32[5,8,256]{2,1,0:T(8,128)S(1)} %get-tuple-element.120), channel_id=1, source_target_pairs={{0,64},{64,128},{128,192},{192,256},{256,320},{320,384},{384,448},... | collective-permute-start | bytes 122888 | tf_op jit(solution)/shard_map/ppermute | solution.py:38
  40.7 7.1 %collective-permute-start.7 = (f32[5,8,256]{2,1,0:T(8,128)S(1)}, f32[5,8,256]{2,1,0:T(8,128)S(1)}, u32[]{:S(2)}, u32[]{:S(2)}) collective-permute-start(f32[5,8,256]{2,1,0:T(8,128)S(1)} %get-tuple-element.119), channel_id=1, source_target_pairs={{64,0},{128,64},{192,128},{256,192},{320,256},{384,320},{448,384},... | collective-permute-start | bytes 122888 | tf_op jit(solution)/shard_map/ppermute | solution.py:38
  47.9 4.4 %collective-permute-start.9 = (f32[5,2,256]{2,1,0:T(2,128)S(1)}, f32[5,2,256]{2,1,0:T(2,128)S(1)}, u32[]{:S(2)}, u32[]{:S(2)}) collective-permute-start(f32[5,2,256]{2,1,0:T(2,128)S(1)} %bitcast.933), channel_id=1, source_target_pairs={{8,0},{16,8},{24,16},{32,24},{40,32},{48,40},{56,48},{9,1},{17,9},... | collective-permute-start | bytes 30728 | tf_op jit(solution)/shard_map/ppermute | solution.py:38
  49.9 5.0 %collective-permute-start.8 = (f32[5,2,256]{2,1,0:T(2,128)S(1)}, f32[5,2,256]{2,1,0:T(2,128)S(1)}, u32[]{:S(2)}, u32[]{:S(2)}) collective-permute-start(f32[5,2,256]{2,1,0:T(2,128)S(1)} %bitcast.937), channel_id=1, source_target_pairs={{0,8},{8,16},{16,24},{24,32},{32,40},{40,48},{48,56},{1,9},{9,17},... | collective-permute-start | bytes 30728 | tf_op jit(solution)/shard_map/ppermute | solution.py:38
  55.1 7.5 %collective-permute-start.10 = (f32[5,2,8]{2,1,0:T(2,128)S(1)}, f32[5,2,8]{2,1,0:T(2,128)S(1)}, u32[]{:S(2)}, u32[]{:S(2)}) collective-permute-start(f32[5,2,8]{2,1,0:T(2,128)S(1)} %slice_reduce_fusion.1), channel_id=1, source_target_pairs={{0,1},{1,2},{2,3},{3,4},{4,5},{5,6},{6,7},{8,9},{9,10},{10,11},{11... | collective-permute-start | bytes 968 | tf_op jit(solution)/shard_map/ppermute | solution.py:38
  60.6 6.7 %collective-permute-start.11 = (f32[5,2,8]{2,1,0:T(2,128)S(1)}, f32[5,2,8]{2,1,0:T(2,128)S(1)}, u32[]{:S(2)}, u32[]{:S(2)}) collective-permute-start(f32[5,2,8]{2,1,0:T(2,128)S(1)} %slice_reduce_fusion), channel_id=1, source_target_pairs={{1,0},{2,1},{3,2},{4,3},{5,4},{6,5},{7,6},{9,8},{10,9},{11,10},{12... | collective-permute-start | bytes 968 | tf_op jit(solution)/shard_map/ppermute | solution.py:38
where the time goes:
time: 70.1 us; the launch traced here: 69.5 us
  starting transfers between devices  36.6 us (52%)
  waiting for transfers between devices  20.2 us (29%)
  local copies, waits for them, and re-layouts  5.53 us (8%)
  other arithmetic  5.31 us (8%)
  between operations  1.85 us (3%)
    ppermute x12, starting transfers between devices, passed_along(): return lax.ppermute(block, axis, route)  36.6 us
    ppermute x12, waiting for transfers between devices, passed_along(): return lax.ppermute(block, axis, route)  20.2 us
    unnamed x47, local copies, waits for them, and re-layouts  3.04 us
    unnamed x84, other arithmetic  1.85 us
  transfers between devices with their start and end apart: 12, of which 6 were waited for; matrix products, arithmetic and copies ran while one was open for 1% of the time, Pallas kernels for 0%

commit v1 on v0

v1 whole, which is shorter than its diff:
```python
import functools

import jax
import jax.numpy as jnp
from jax import lax
from jax.experimental import pallas as pl
from jax.experimental.pallas import tpu as pltpu
from jax.sharding import PartitionSpec as P

VELOCITIES = [
    (0, 0, 0),
    (1, 0, 0),
    (-1, 0, 0),
    (0, 1, 0),
    (0, -1, 0),
    (0, 0, 1),
    (0, 0, -1),
    (1, 1, 0),
    (-1, -1, 0),
    (1, -1, 0),
    (-1, 1, 0),
    (1, 0, 1),
    (-1, 0, -1),
    (1, 0, -1),
    (-1, 0, 1),
    (0, 1, 1),
    (0, -1, -1),
    (0, 1, -1),
    (0, -1, 1),
]
WEIGHTS = [1.0 / 3.0] + [1.0 / 18.0] * 6 + [1.0 / 36.0] * 12
AXES = ("gx", "gy", "gz")
MESH = pl.DeviceIdType.MESH

FACES = [v for v in VELOCITIES if sum(map(abs, v)) == 1]
EDGES = [v for v in VELOCITIES if sum(map(abs, v)) == 2]
DIRECTIONS = FACES + EDGES
X_POPS = {s: [i for i, v in enumerate(VELOCITIES) if v[0] == s] for s in (1, -1)}


def side(sign):
    return 0 if sign == 1 else 1


def crossing(axis, sign):
    inside, corner = [], []
    for i, v in enumerate(VELOCITIES):
        if v[axis] != sign:
            continue
        for plane in (0, 1):
            (inside if 0 <= plane + v[0] <= 1 else corner).append((i, plane))
    return inside + sorted(corner, key=lambda pair: -VELOCITIES[pair[0]][0])


Y_SLOTS = {s: crossing(1, s) for s in (1, -1)}
Z_SLOTS = {s: crossing(2, s) for s in (1, -1)}


def slot_of(slots, sign, i, plane):
    return slots[sign].index((i, plane))


def kernel(
    sizes, dist_hbm, kinds_hbm, relax_hbm, inflow_hbm, rho_ref, mom_ref,
    field, kinds, relax, inflow, post, xs1, xs2, xr1, xr2, ys, yr, xyr, zs, zr, xzr, yzr,
    load_sem, send_sem, recv_sem,
):
    me = tuple(lax.axis_index(a) for a in AXES)
    exists = {}
    for axis in range(3):
        exists[axis, 1] = me[axis] < sizes[axis] - 1
        exists[axis, -1] = me[axis] > 0

    def has(direction):
        parts = [exists[a, s] for a, s in enumerate(direction) if s != 0]
        return parts[0] if len(parts) == 1 else jnp.logical_and(parts[0], parts[1])

    def target(direction):
        return tuple(m + s for m, s in zip(me, direction))

    def opposite(direction):
        return tuple(-s for s in direction)

    loads = []
    for plane in (1, 0):
        group = [
            pltpu.make_async_copy(dist_hbm.at[:, plane], field.at[:, plane], load_sem.at[plane, 0]),
            pltpu.make_async_copy(kinds_hbm.at[plane], kinds.at[plane], load_sem.at[plane, 1]),
            pltpu.make_async_copy(relax_hbm.at[plane], relax.at[plane], load_sem.at[plane, 2]),
            pltpu.make_async_copy(inflow_hbm.at[:, plane], inflow.at[:, plane], load_sem.at[plane, 3]),
        ]
        for copy in group:
            copy.start()
        loads.append(group)

    barrier = pltpu.get_barrier_semaphore()
    neighbours = 0
    for d in DIRECTIONS:
        present = has(d)
        neighbours = neighbours + present.astype(jnp.int32)

        @pl.when(present)
        def _():
            pl.semaphore_signal(barrier, inc=1, device_id=target(d), device_id_type=MESH)

    def message(step, d):
        dx, dy, dz = d
        if dy == 0 and dz == 0:
            return ((xs1, xr1), (xs2, xr2))[step][0].at[side(dx)], ((xs1, xr1), (xs2, xr2))[step][1].at[side(dx)]
        if dz == 0 and dx == 0:
            return ys.at[step, side(dy), 0:8], yr.at[step, side(dy)]
        if dx == 0 and dy == 0:
            return zs.at[step, side(dz)], zr.at[step, side(dz)]
        if dz == 0:
            row = 8 + side(dx)
            return ys.at[step, side(dy), row : row + 1], xyr.at[step, side(dx), side(dy), 0:1]
        if dy == 0:
            return zs.at[step, side(dz)], xzr.at[step, side(dx), side(dz)]
        row = 7 if dy == 1 else 0
        return zs.at[step, side(dz), row : row + 1], yzr.at[step, side(dy), side(dz), 0:1]

    def copy_of(step, d):
        src, dst = message(step, d)
        k = DIRECTIONS.index(d)
        return pltpu.make_async_remote_copy(
            src_ref=src, dst_ref=dst, send_sem=send_sem.at[step, k], recv_sem=recv_sem.at[step, k],
            device_id=target(d), device_id_type=MESH,
        )

    def send(step, d):
        @pl.when(has(d))
        def _():
            copy_of(step, d).start()

    def received(step, d):
        @pl.when(has(opposite(d)))
        def _():
            copy_of(step, d).wait_recv()

    for d in DIRECTIONS:
        @pl.when(jnp.logical_not(has(opposite(d))))
        def _():
            for step in (0, 1):
                dst = message(step, d)[1]
                dst[...] = jnp.zeros(dst.shape, jnp.float32)

    row_id = lax.broadcasted_iota(jnp.int32, (8, 128), 0)
    lane_id = lax.broadcasted_iota(jnp.int32, (8, 128), 1)

    def halves(ref, *index):
        return [ref[index + (slice(None), slice(h * 128, h * 128 + 128))] for h in (0, 1)]

    def collide(plane):
        for h in (0, 1):
            z = slice(h * 128, h * 128 + 128)
            f = [field[i, plane, :, z] for i in range(19)]
            rho = f[0]
            for i in range(1, 19):
                rho = rho + f[i]
            u = []
            for axis in range(3):
                plus = [f[i] for i in range(19) if VELOCITIES[i][axis] == 1]
                minus = [f[i] for i in range(19) if VELOCITIES[i][axis] == -1]
                u.append(functools.reduce(jnp.add, plus) - functools.reduce(jnp.add, minus))
            kind = kinds[plane, :, z]
            wall, fluid, inlet, outlet = kind == 0, kind == 1, kind == 2, kind == 3
            one = jnp.ones((8, 128), jnp.float32)
            r = jnp.where(jnp.logical_or(wall, jnp.logical_or(fluid, inlet)), rho, one)
            v = [jnp.where(inlet, inflow[a, plane, :, z], u[a]) for a in range(3)]
            take = jnp.where(wall, jnp.zeros_like(one), jnp.where(fluid, relax[plane, :, z], one))
            keep = one - take
            usq = v[0] * v[0] + v[1] * v[1] + v[2] * v[2]
            common = r - 1.5 * usq
            post[0, plane, :, z] = keep * f[0] + take * (WEIGHTS[0] * common)
            for i in range(1, 19, 2):
                c = VELOCITIES[i]
                along = None
                for a in range(3):
                    if c[a] != 0:
                        term = v[a] if c[a] == 1 else -v[a]
                        along = term if along is None else along + term
                even = WEIGHTS[i] * (common + 4.5 * along * along)
                odd = (3.0 * WEIGHTS[i]) * along
                here = jnp.where(wall, f[i + 1], f[i])
                there = jnp.where(wall, f[i], f[i + 1])
                post[i, plane, :, z] = keep * here + take * (even + odd)
                post[i + 1, plane, :, z] = keep * there + take * (even - odd)

    def pack(step):
        for s in (1, -1):
            tile = None
            for k, (i, plane) in enumerate(Z_SLOTS[s]):
                if s == 1:
                    col = pltpu.roll(post[i, plane, :, 128:256], (1 + k) % 128, 1)
                    at = k
                else:
                    col = pltpu.roll(post[i, plane, :, 0:128], (127 - k) % 128, 1)
                    at = 127 - k
                tile = col if tile is None else jnp.where(lane_id == at, col, tile)
            zs[step, side(s)] = tile
            row = 7 if s == 1 else 0
            for k, (i, plane) in enumerate(Y_SLOTS[s]):
                ys[step, side(s), k : k + 1] = post[i, plane, row : row + 1]

    def y_moved(planes, sign, edge_row):
        out = []
        for h in (0, 1):
            rolled = pltpu.roll(planes[h], sign % 8, 0)
            edge = 0 if sign == 1 else 7
            out.append(jnp.where(row_id == edge, edge_row[h], rolled))
        return out

    def z_moved(planes, sign, edge_tile):
        rolled = [pltpu.roll(p, sign % 128, 1) for p in planes]
        if sign == 1:
            at = lane_id == 0
            return [jnp.where(at, edge_tile, rolled[0]), jnp.where(at, rolled[0], rolled[1])]
        at = lane_id == 127
        return [jnp.where(at, rolled[1], rolled[0]), jnp.where(at, edge_tile, rolled[1])]

    def z_column(tile, sign, k):
        shift = (128 - k) % 128 if sign == 1 else k % 128
        return tile if shift == 0 else pltpu.roll(tile, shift, 1)

    def inside(step, i, plane):
        cx, cy, cz = VELOCITIES[i]
        q = plane - cx
        value = halves(post, i, q)
        if cy != 0:
            k = slot_of(Y_SLOTS, cy, i, q)
            row = [yr[step, side(cy), k : k + 1, h * 128 : h * 128 + 128] for h in (0, 1)]
            value = y_moved(value, cy, row)
        if cz != 0:
            tile = zr[step, side(cz)]
            if cy != 0:
                edge = 0 if cy == 1 else 7
                tile = jnp.where(row_id == edge, yzr[step, side(cy), side(cz), 0:1], pltpu.roll(tile, cy % 8, 0))
            value = z_moved(value, cz, z_column(tile, cz, slot_of(Z_SLOTS, cz, i, q)))
        return value

    def x_plane(cx):
        return 0 if cx == 1 else 1

    def put(i, plane, value):
        for h in (0, 1):
            field[i, plane, :, h * 128 : h * 128 + 128] = value[h]

    for plane, group in zip((1, 0), loads):
        for copy in group:
            copy.wait()
        collide(plane)
    for s in (1, -1):
        for k, i in enumerate(X_POPS[s]):
            xs1[side(s), k] = post[i, 1 - x_plane(s)]
    pack(0)
    pl.semaphore_wait(barrier, neighbours)
    order = [d for d in EDGES if d[0] != 0] + FACES[:2] + [d for d in EDGES if d[0] == 0] + FACES[2:]
    for d in order:
        send(0, d)

    for d in FACES[2:] + [d for d in EDGES if d[0] == 0]:
        received(0, d)
    for i in range(19):
        for plane in (0, 1):
            if 0 <= plane - VELOCITIES[i][0] <= 1:
                put(i, plane, inside(0, i, plane))
    for d in [d for d in EDGES if d[0] != 0] + FACES[:2]:
        received(0, d)
    for s in (1, -1):
        for n, i in enumerate(X_POPS[s]):
            _, cy, cz = VELOCITIES[i]
            value = halves(xr1, side(s), n)
            if cy != 0:
                row = [xyr[0, side(s), side(cy), 0:1, h * 128 : h * 128 + 128] for h in (0, 1)]
                value = y_moved(value, cy, row)
            if cz != 0:
                k = slot_of(Z_SLOTS, cz, i, 1 - x_plane(s))
                value = z_moved(value, cz, z_column(xzr[0, side(s), side(cz)], cz, k))
            put(i, x_plane(s), value)

    for plane in (1, 0):
        collide(plane)
    zero = jnp.zeros((8, 128), jnp.float32)
    zero_row = [jnp.zeros((1, 128), jnp.float32)] * 2
    for s in (1, -1):
        source = 1 - x_plane(s)
        total, moment_y, moment_z = None, None, None
        for i in X_POPS[s]:
            _, cy, cz = VELOCITIES[i]
            value = halves(post, i, source)
            if cy != 0:
                value = y_moved(value, cy, zero_row)
                moment_y = value if moment_y is None else [a - b for a, b in zip(moment_y, value)]
                flip_y = cy if moment_y is value else flip_y
            if cz != 0:
                value = z_moved(value, cz, zero)
                moment_z = value if moment_z is None else [a - b for a, b in zip(moment_z, value)]
                flip_z = cz if moment_z is value else flip_z
            total = value if total is None else [a + b for a, b in zip(total, value)]
        if flip_y == -1:
            moment_y = [-a for a in moment_y]
        if flip_z == -1:
            moment_z = [-a for a in moment_z]
        for n, value in enumerate((total, moment_y, moment_z)):
            for h in (0, 1):
                xs2[side(s), n, :, h * 128 : h * 128 + 128] = value[h]
    pack(1)
    for d in order:
        send(1, d)

    for d in FACES[2:] + [d for d in EDGES if d[0] == 0]:
        received(1, d)
    sums = []
    for plane in (0, 1):
        acc = [[zero, zero] for _ in range(4)]
        for i in range(19):
            c = VELOCITIES[i]
            if not 0 <= plane - c[0] <= 1:
                continue
            value = inside(1, i, plane)
            for h in (0, 1):
                acc[0][h] = acc[0][h] + value[h]
                for a in range(3):
                    if c[a] == 1:
                        acc[1 + a][h] = acc[1 + a][h] + value[h]
                    if c[a] == -1:
                        acc[1 + a][h] = acc[1 + a][h] - value[h]
        sums.append(acc)
    for d in [d for d in EDGES if d[0] != 0] + FACES[:2]:
        received(1, d)
    for s in (1, -1):
        plane = x_plane(s)
        acc = sums[plane]
        for h in (0, 1):
            z = slice(h * 128, h * 128 + 128)
            total, moment_y, moment_z = (xr2[side(s), n, :, z] for n in range(3))
            for cy in (1, -1):
                edge = 0 if cy == 1 else 7
                value = jnp.where(row_id == edge, xyr[1, side(s), side(cy), 0:1, z], zero)
                total = total + value
                moment_y = moment_y + value if cy == 1 else moment_y - value
            for cz in (1, -1):
                if h != (0 if cz == 1 else 1):
                    continue
                i = VELOCITIES.index((s, 0, cz))
                column = z_column(xzr[1, side(s), side(cz)], cz, slot_of(Z_SLOTS, cz, i, 1 - plane))
                value = jnp.where(lane_id == (0 if cz == 1 else 127), column, zero)
                total = total + value
                moment_z = moment_z + value if cz == 1 else moment_z - value
            rho_ref[plane, :, z] = acc[0][h] + total
            mom_ref[0, plane, :, z] = acc[1][h] + total if s == 1 else acc[1][h] - total
            mom_ref[1, plane, :, z] = acc[2][h] + moment_y
            mom_ref[2, plane, :, z] = acc[3][h] + moment_z

    for step in (0, 1):
        for d in DIRECTIONS:
            @pl.when(has(d))
            def _():
                copy_of(step, d).wait_send()


def solution(mesh):
    sizes = tuple(mesh.shape[a] for a in AXES)

    def shards(dist, site_kinds, relax, inflow):
        f32 = jnp.float32
        block = site_kinds.shape
        return pl.pallas_call(
            functools.partial(kernel, sizes),
            out_shape=(
                jax.ShapeDtypeStruct(block, f32),
                jax.ShapeDtypeStruct((3,) + block, f32),
            ),
            in_specs=[pl.BlockSpec(memory_space=pl.ANY)] * 4,
            out_specs=(pl.BlockSpec(memory_space=pltpu.VMEM), pl.BlockSpec(memory_space=pltpu.VMEM)),
            scratch_shapes=[
                pltpu.VMEM((19,) + block, f32),
                pltpu.VMEM(block, jnp.int32),
                pltpu.VMEM(block, f32),
                pltpu.VMEM((3,) + block, f32),
                pltpu.VMEM((19,) + block, f32),
                pltpu.VMEM((2, 5, 8, 256), f32),
                pltpu.VMEM((2, 3, 8, 256), f32),
                pltpu.VMEM((2, 5, 8, 256), f32),
                pltpu.VMEM((2, 3, 8, 256), f32),
                pltpu.VMEM((2, 2, 16, 256), f32),
                pltpu.VMEM((2, 2, 8, 256), f32),
                pltpu.VMEM((2, 2, 2, 8, 256), f32),
                pltpu.VMEM((2, 2, 8, 128), f32),
                pltpu.VMEM((2, 2, 8, 128), f32),
                pltpu.VMEM((2, 2, 2, 8, 128), f32),
                pltpu.VMEM((2, 2, 2, 8, 128), f32),
                pltpu.SemaphoreType.DMA((2, 4)),
                pltpu.SemaphoreType.DMA((2, 18)),
                pltpu.SemaphoreType.DMA((2, 18)),
            ],
            compiler_params=pltpu.CompilerParams(collective_id=0, has_side_effects=True),
        )(dist, site_kinds, relax, inflow)

    return jax.shard_map(
        shards,
        mesh=mesh,
        in_specs=(
            P(None, "gx", "gy", "gz"),
            P("gx", "gy", "gz"),
            P("gx", "gy", "gz"),
            P(None, "gx", "gy", "gz"),
        ),
        out_specs=(P("gx", "gy", "gz"), P(None, "gx", "gy", "gz")),
        check_vma=False,
    )
```

time: 70.1 us -> 27.2 us (0.39)
  the two profiles are of different devices: /device:TPU:346 before, /device:TPU:1 now
where the time goes in v1:
time: 27.2 us; the launch traced here: 26.9 us
  Pallas kernels  23.6 us (87%)
  local copies, waits for them, and re-layouts  2.74 us (10%)
  between operations  0.64 us (2%)
    pallas_call x1, Pallas kernels, shards(): pl.pallas_call(functools.partial(kernel, sizes), out_shape=(jax.ShapeDtyp...  23.6 us
    unnamed x2, local copies, waits for them, and re-layouts  2.74 us

profile of v1, /device:TPU:1, one launch (start us, length us, event | category | flops | bytes accessed | tf_op | source)
XLA Modules:
  0.0 26.9 jit_solution(10888279166542309258)
XLA Ops:
  0.6 23.6 %shard_map.59 = (f32[2,8,256]{2,1,0:T(8,128)}, f32[3,2,8,256]{3,2,1,0:T(8,128)}) custom-call(f32[19,2,8,256]{3,2,1,0:T(8,128)} %dist_hbm.1, s32[2,8,256]{2,1,0:T(8,128)} %kinds_hbm.1, f32[2,8,256]{2,1,0:T(8,128)} %relax_hbm.1, f32[3,2,8,256]{3,2,1,0:T(8,128)} %inflow_hbm.1), custom_call_target="tpu_custom_call" | custom-call | tf_op jit(solution)/shard_map/pallas_call | solution.py:368
  24.2 1.3 %copy.8 = f32[2,8,256]{2,1,0:T(8,128)} copy(f32[2,8,256]{2,1,0:T(8,128)} %get-tuple-element.4) | data formatting | bytes 32768
  25.5 1.4 %copy.9 = f32[3,2,8,256]{3,2,1,0:T(8,128)} copy(f32[3,2,8,256]{3,2,1,0:T(8,128)} %get-tuple-element.5) | data formatting | bytes 98304

commit v2 on v1

--- a/solution.py
+++ b/solution.py
@@ -61,9 +61,9 @@
 
 
 def kernel(
-    sizes, dist_hbm, kinds_hbm, relax_hbm, inflow_hbm, rho_ref, mom_ref,
+    sizes, dist_hbm, kinds_hbm, relax_hbm, inflow_hbm, out_ref,
     field, kinds, relax, inflow, post, xs1, xs2, xr1, xr2, ys, yr, xyr, zs, zr, xzr, yzr,
-    load_sem, send_sem, recv_sem,
+    load_sem, send_sem, recv_sem, entered,
 ):
     me = tuple(lax.axis_index(a) for a in AXES)
     exists = {}
@@ -93,15 +93,37 @@
             copy.start()
         loads.append(group)
 
+    def is_origin(place):
+        return jnp.logical_and(place[0] == 0, jnp.logical_and(place[1] == 0, place[2] == 0))
+
+    here_origin = is_origin(me)
+
+    def upward(d):
+        return next(s for s in (d[0], d[2], d[1]) if s != 0) == 1
+
+    def later(d):
+        if upward(d):
+            return jnp.logical_and(has(d), jnp.logical_not(here_origin))
+        if max(d) == 1:
+            return None
+        return is_origin(target(d))
+
+    def earlier(d):
+        if upward(d):
+            return jnp.logical_and(has(d), here_origin)
+        if max(d) == 1:
+            return has(d)
+        return jnp.logical_and(has(d), jnp.logical_not(is_origin(target(d))))
+
     barrier = pltpu.get_barrier_semaphore()
-    neighbours = 0
     for d in DIRECTIONS:
-        present = has(d)
-        neighbours = neighbours + present.astype(jnp.int32)
-
-        @pl.when(present)
-        def _():
-            pl.semaphore_signal(barrier, inc=1, device_id=target(d), device_id_type=MESH)
+        if later(d) is not None:
+            @pl.when(later(d))
+            def _():
+                pl.semaphore_signal(barrier, inc=1, device_id=target(d), device_id_type=MESH)
+    before = 0
+    for d in DIRECTIONS:
+        before = before + earlier(d).astype(jnp.int32)
 
     def message(step, d):
         dx, dy, dz = d
@@ -131,6 +153,12 @@
         @pl.when(has(d))
         def _():
             copy_of(step, d).start()
+
+    def send_later(d):
+        @pl.when(later(d))
+        def _():
+            pl.semaphore_wait(entered.at[DIRECTIONS.index(d)], 1)
+            copy_of(0, d).start()
 
     def received(step, d):
         @pl.when(has(opposite(d)))
@@ -245,6 +273,16 @@
         for h in (0, 1):
             field[i, plane, :, h * 128 : h * 128 + 128] = value[h]
 
+    @pl.when(before > 0)
+    def _():
+        pl.semaphore_wait(barrier, before)
+
+    for d in DIRECTIONS:
+        @pl.when(earlier(d))
+        def _():
+            at = entered.at[DIRECTIONS.index(opposite(d))]
+            pl.semaphore_signal(at, inc=1, device_id=target(d), device_id_type=MESH)
+
     for plane, group in zip((1, 0), loads):
         for copy in group:
             copy.wait()
@@ -253,10 +291,17 @@
         for k, i in enumerate(X_POPS[s]):
             xs1[side(s), k] = post[i, 1 - x_plane(s)]
     pack(0)
-    pl.semaphore_wait(barrier, neighbours)
     order = [d for d in EDGES if d[0] != 0] + FACES[:2] + [d for d in EDGES if d[0] == 0] + FACES[2:]
     for d in order:
-        send(0, d)
+        @pl.when(earlier(d))
+        def _():
+            copy_of(0, d).start()
+    for d in order:
+        if upward(d):
+            send_later(d)
+    for d in order:
+        if max(d) < 1:
+            send_later(d)
 
     for d in FACES[2:] + [d for d in EDGES if d[0] == 0]:
         received(0, d)
@@ -347,10 +392,10 @@
                 value = jnp.where(lane_id == (0 if cz == 1 else 127), column, zero)
                 total = total + value
                 moment_z = moment_z + value if cz == 1 else moment_z - value
-            rho_ref[plane, :, z] = acc[0][h] + total
-            mom_ref[0, plane, :, z] = acc[1][h] + total if s == 1 else acc[1][h] - total
-            mom_ref[1, plane, :, z] = acc[2][h] + moment_y
-            mom_ref[2, plane, :, z] = acc[3][h] + moment_z
+            out_ref[0, plane, :, z] = acc[0][h] + total
+            out_ref[1, plane, :, z] = acc[1][h] + total if s == 1 else acc[1][h] - total
+            out_ref[2, plane, :, z] = acc[2][h] + moment_y
+            out_ref[3, plane, :, z] = acc[3][h] + moment_z
 
     for step in (0, 1):
         for d in DIRECTIONS:
@@ -359,20 +404,28 @@
                 copy_of(step, d).wait_send()
 
 
+def finish(sums_ref, rho_hbm, mom_hbm, sems):
+    copies = [
+        pltpu.make_async_copy(sums_ref.at[0], rho_hbm, sems.at[0]),
+        pltpu.make_async_copy(sums_ref.at[1:4], mom_hbm, sems.at[1]),
+    ]
+    for copy in copies:
+        copy.start()
+    for copy in copies:
+        copy.wait()
+
+
 def solution(mesh):
     sizes = tuple(mesh.shape[a] for a in AXES)
 
     def shards(dist, site_kinds, relax, inflow):
         f32 = jnp.float32
         block = site_kinds.shape
-        return pl.pallas_call(
+        sums = pl.pallas_call(
             functools.partial(kernel, sizes),
-            out_shape=(
-                jax.ShapeDtypeStruct(block, f32),
-                jax.ShapeDtypeStruct((3,) + block, f32),
-            ),
+            out_shape=pltpu.VMEM((4,) + block, f32),
             in_specs=[pl.BlockSpec(memory_space=pl.ANY)] * 4,
-            out_specs=(pl.BlockSpec(memory_space=pltpu.VMEM), pl.BlockSpec(memory_space=pltpu.VMEM)),
+            out_specs=pl.BlockSpec(memory_space=pltpu.VMEM),
             scratch_shapes=[
                 pltpu.VMEM((19,) + block, f32),
                 pltpu.VMEM(block, jnp.int32),
@@ -393,9 +446,20 @@
                 pltpu.SemaphoreType.DMA((2, 4)),
                 pltpu.SemaphoreType.DMA((2, 18)),
                 pltpu.SemaphoreType.DMA((2, 18)),
+                pltpu.SemaphoreType.REGULAR((18,)),
             ],
             compiler_params=pltpu.CompilerParams(collective_id=0, has_side_effects=True),
         )(dist, site_kinds, relax, inflow)
+        return pl.pallas_call(
+            finish,
+            out_shape=(
+                jax.ShapeDtypeStruct(block, f32),
+                jax.ShapeDtypeStruct((3,) + block, f32),
+            ),
+            in_specs=[pl.BlockSpec(memory_space=pltpu.VMEM)],
+            out_specs=(pl.BlockSpec(memory_space=pl.ANY), pl.BlockSpec(memory_space=pl.ANY)),
+            scratch_shapes=[pltpu.SemaphoreType.DMA((2,))],
+        )(pltpu.with_memory_space_constraint(sums, pltpu.VMEM))
 
     return jax.shard_map(
         shards,

time: 27.2 us -> 23.9 us (0.88)
  local copies, waits for them, and re-layouts: 2.74 us -> 0 us
  Pallas kernels: 23.6 us -> 23.1 us
    unnamed x2 -> x0, local copies, waits for them, and re-layouts: 2.74 us -> none
    pallas_call x1 -> x2, Pallas kernels: 23.6 us -> 23.1 us  [the longest x1 22.4 us: shards(): pl.pallas_call(functools.partial(kernel, sizes), out_shape=pltpu.VMEM((4,...]
where the time goes in v2:
time: 23.9 us; the launch traced here: 23.7 us
  Pallas kernels  23.1 us (97%)
  between operations  0.64 us (3%)
    pallas_call x1, Pallas kernels, shards(): pl.pallas_call(functools.partial(kernel, sizes), out_shape=pltpu.VMEM((4,...  22.4 us
    pallas_call x1, Pallas kernels, shards(): pl.pallas_call(finish, out_shape=(jax.ShapeDtypeStruct(block, f32), jax.S...  0.65 us

profile of v2, /device:TPU:1, one launch (start us, length us, event | category | flops | bytes accessed | tf_op | source)
XLA Modules:
  0.0 23.7 jit_solution(2700451573071280983)
XLA Ops:
  0.6 22.4 %shard_map.59.sums_ref = f32[4,2,8,256]{3,2,1,0:T(8,128)S(1)} custom-call(f32[19,2,8,256]{3,2,1,0:T(8,128)} %dist_hbm.1, s32[2,8,256]{2,1,0:T(8,128)} %kinds_hbm.1, f32[2,8,256]{2,1,0:T(8,128)} %relax_hbm.1, f32[3,2,8,256]{3,2,1,0:T(8,128)} %inflow_hbm.1), custom_call_target="tpu_custom_call" | custom-call | tf_op jit(solution)/shard_map/pallas_call | solution.py:424
  23.1 0.6 %shard_map.60 = (f32[2,8,256]{2,1,0:T(8,128)}, f32[3,2,8,256]{3,2,1,0:T(8,128)}) custom-call(f32[4,2,8,256]{3,2,1,0:T(8,128)S(1)} %shard_map.59.sums_ref), custom_call_target="tpu_custom_call" | custom-call | tf_op jit(solution)/shard_map/pallas_call | solution.py:453

commit v3 on v0

v3 whole, which is shorter than its diff:
```python
import functools

import jax
import jax.numpy as jnp
from jax import lax
from jax.experimental import pallas as pl
from jax.experimental.pallas import tpu as pltpu
from jax.sharding import PartitionSpec as P

VELOCITIES = [
    (0, 0, 0),
    (1, 0, 0),
    (-1, 0, 0),
    (0, 1, 0),
    (0, -1, 0),
    (0, 0, 1),
    (0, 0, -1),
    (1, 1, 0),
    (-1, -1, 0),
    (1, -1, 0),
    (-1, 1, 0),
    (1, 0, 1),
    (-1, 0, -1),
    (1, 0, -1),
    (-1, 0, 1),
    (0, 1, 1),
    (0, -1, -1),
    (0, 1, -1),
    (0, -1, 1),
]
WEIGHTS = [1.0 / 3.0] + [1.0 / 18.0] * 6 + [1.0 / 36.0] * 12
AXES = ("gx", "gy", "gz")
MESH = pl.DeviceIdType.MESH

KIND, RELAX, INFLOW = 19, 20, 21
VEL = VELOCITIES + [(0, 0, 0)] * 5
FIELDS = range(24)
ORDER = sorted(FIELDS, key=lambda j: (-VEL[j][0], j))
POS = [ORDER.index(j) for j in FIELDS]
STEPS = (-1, 0, 1)
DIRECTIONS = [(x, y, z) for x in STEPS for y in STEPS for z in STEPS if (x, y, z) != (0, 0, 0)]
NEAR = (-1, 0, 1, 2)


def groups(axis, sign):
    found = [(j, 1) for j in FIELDS if VEL[j][axis] in (0, sign)]
    found += [(j, 2) for j in FIELDS if VEL[j][axis] == sign]
    return sorted(found, key=lambda pair: VEL[pair[0]][0])


ROWS = {s: groups(1, s) for s in (1, -1)}
COLS = {s: groups(2, s) for s in (1, -1)}
LOCAL = {s: sorted([j for j in FIELDS if VEL[j][2] == -s], key=lambda j: VEL[j][0]) for s in (1, -1)}
LOCAL_LANE = {1: 96, -1: 64}


def side(sign):
    return 0 if sign == 1 else 1


def opposite(direction):
    return tuple(-s for s in direction)


def upward(d):
    return next(s for s in (d[0], d[2], d[1]) if s != 0) == 1


def messages():
    found = []
    for d in DIRECTIONS:
        dx, dy, dz = d
        if dy == 0 and dz == 0:
            found += [("xp", d), ("xb", d), ("xa", d)]
        if dz == 0 and dy != 0:
            found.append(("y", d))
        if dz != 0:
            found.append(("z", d))
        else:
            found.append(("l", d))
    return found


MESSAGES = messages()


def kernel(
    sizes, dist_hbm, kinds_hbm, relax_hbm, inflow_hbm, out_ref,
    field, kinds, block, ys, yr, zs, zr, ls, lr, first, second, row_tile, row_post,
    load_sem, send_sem, recv_sem, entered,
):
    me = tuple(lax.axis_index(a) for a in AXES)
    exists = {}
    for axis in range(3):
        exists[axis, 1] = me[axis] < sizes[axis] - 1
        exists[axis, -1] = me[axis] > 0

    def has(direction):
        parts = [exists[a, s] for a, s in enumerate(direction) if s != 0]
        return functools.reduce(jnp.logical_and, parts)

    def target(direction):
        return tuple(m + s for m, s in zip(me, direction))

    loads = []
    for p in (1, 0):
        group = [
            pltpu.make_async_copy(kinds_hbm.at[p], kinds.at[p], load_sem.at[p, 0]),
            pltpu.make_async_copy(relax_hbm.at[p], block.at[POS[RELAX], 2 + p], load_sem.at[p, 1]),
            pltpu.make_async_copy(
                inflow_hbm.at[:, p], block.at[POS[INFLOW] : POS[INFLOW] + 3, 2 + p], load_sem.at[p, 2]
            ),
            pltpu.make_async_copy(dist_hbm.at[:, p], field.at[:, p], load_sem.at[p, 3]),
        ]
        for copy in group:
            copy.start()
        loads.append(group)

    def is_origin(place):
        return jnp.logical_and(place[0] == 0, jnp.logical_and(place[1] == 0, place[2] == 0))

    here_origin = is_origin(me)

    def later(d):
        if upward(d):
            return jnp.logical_and(has(d), jnp.logical_not(here_origin))
        if max(d) == 1:
            return None
        return is_origin(target(d))

    def earlier(d):
        if upward(d):
            return jnp.logical_and(has(d), here_origin)
        if max(d) == 1:
            return has(d)
        return jnp.logical_and(has(d), jnp.logical_not(is_origin(target(d))))

    barrier = pltpu.get_barrier_semaphore()
    for d in DIRECTIONS:
        if later(d) is not None:
            @pl.when(later(d))
            def _():
                pl.semaphore_signal(barrier, inc=1, device_id=target(d), device_id_type=MESH)
    before = 0
    for d in DIRECTIONS:
        before = before + earlier(d).astype(jnp.int32)

    def ends(m):
        kind, (dx, dy, dz) = m
        if kind == "xa":
            at, mine, theirs = (slice(0, 5), slice(2, 4), slice(0, 2)) if dx == 1 else (slice(19, 24), slice(2, 4), slice(4, 6))
            return block.at[at, mine], block.at[at, theirs]
        if kind in ("xb", "xp"):
            at = slice(5, 14) if kind == "xb" else slice(14, 19)
            mine, theirs = (3, 1) if dx == 1 else (2, 4)
            return block.at[at, mine : mine + 1], block.at[at, theirs : theirs + 1]
        if kind == "y":
            rows = {0: slice(0, 48), 1: slice(8, 48), -1: slice(0, 40)}[dx]
            return ys.at[side(dy), rows], yr.at[side(dy), dx + 1, rows]
        if kind == "z":
            return zs.at[side(dz)], zr.at[side(dz), dx + 1, dy + 1]
        return ls.at[0], lr.at[dx + 1, dy + 1]

    def copy_of(m):
        src, dst = ends(m)
        k = MESSAGES.index(m)
        return pltpu.make_async_remote_copy(
            src_ref=src, dst_ref=dst, send_sem=send_sem.at[k], recv_sem=recv_sem.at[k],
            device_id=target(m[1]), device_id_type=MESH,
        )

    for m in MESSAGES:
        @pl.when(jnp.logical_not(has(opposite(m[1]))))
        def _():
            dst = ends(m)[1]
            dst[...] = jnp.zeros(dst.shape, jnp.float32)

    row_id = lax.broadcasted_iota(jnp.int32, (8, 128), 0)
    lane_id = lax.broadcasted_iota(jnp.int32, (8, 128), 1)
    one = jnp.ones((8, 128), jnp.float32)
    zero = jnp.zeros((8, 128), jnp.float32)

    def turn(tile, shift):
        shift %= 128
        return tile if shift == 0 else pltpu.roll(tile, shift, 1)

    def slide(tile, shift):
        return pltpu.roll(tile, shift % 8, 0)

    def lanes(h):
        return slice(h * 128, h * 128 + 128)

    def collide(f, kind, relax, inflow, wanted, inside=None):
        rho = functools.reduce(jnp.add, f)
        u = []
        for axis in range(3):
            plus = [f[i] for i in range(19) if VELOCITIES[i][axis] == 1]
            minus = [f[i] for i in range(19) if VELOCITIES[i][axis] == -1]
            u.append(functools.reduce(jnp.add, plus) - functools.reduce(jnp.add, minus))
        wall, fluid = kind < 0.5, jnp.logical_and(kind > 0.5, kind < 1.5)
        inlet, outlet = jnp.logical_and(kind > 1.5, kind < 2.5), kind > 2.5
        r = jnp.where(outlet, one, rho)
        v = [jnp.where(inlet, inflow[a], u[a]) for a in range(3)]
        take = jnp.where(wall, zero, jnp.where(fluid, relax, one))
        keep = one - take
        if inside is not None:
            take, keep = take * inside, keep * inside
        usq = v[0] * v[0] + v[1] * v[1] + v[2] * v[2]
        common = r - 1.5 * usq
        post = {}
        if 0 in wanted:
            post[0] = keep * f[0] + take * (WEIGHTS[0] * common)
        for i in range(1, 19, 2):
            if i not in wanted and i + 1 not in wanted:
                continue
            along = None
            for a in range(3):
                if VELOCITIES[i][a] != 0:
                    term = v[a] if VELOCITIES[i][a] == 1 else -v[a]
                    along = term if along is None else along + term
            even = WEIGHTS[i] * (common + 4.5 * along * along)
            odd = (3.0 * WEIGHTS[i]) * along
            if i in wanted:
                post[i] = keep * jnp.where(wall, f[i + 1], f[i]) + take * (even + odd)
            if i + 1 in wanted:
                post[i + 1] = keep * jnp.where(wall, f[i], f[i + 1]) + take * (even - odd)
        return post

    def send_when(m, condition):
        @pl.when(condition)
        def _():
            copy_of(m).start()

    @pl.when(before > 0)
    def _():
        pl.semaphore_wait(barrier, before)

    for d in DIRECTIONS:
        @pl.when(earlier(d))
        def _():
            at = entered.at[DIRECTIONS.index(opposite(d))]
            pl.semaphore_signal(at, inc=1, device_id=target(d), device_id_type=MESH)

    for p, group in zip((1, 0), loads):
        for copy in group[:3]:
            copy.wait()
        block[POS[KIND], 2 + p] = kinds[p].astype(jnp.float32)
        for m in MESSAGES:
            if m[0] == "xp" and m[1][0] == (1 if p == 1 else -1):
                send_when(m, earlier(m[1]))
        group[3].wait()
        for h in (0, 1):
            z = lanes(h)
            post = collide(
                [field[i, p, :, z] for i in range(19)],
                block[POS[KIND], 2 + p, :, z],
                block[POS[RELAX], 2 + p, :, z],
                [block[POS[INFLOW + a], 2 + p, :, z] for a in range(3)],
                range(19),
            )
            for i in range(19):
                block[POS[i], 2 + p, :, z] = post[i]

    def column(j, p, at):
        return block[POS[j], 2 + p, :, lanes(at // 128)], at % 128

    for s in (1, -1):
        tile = zero
        for g, (j, depth) in enumerate(COLS[s]):
            for p in (0, 1):
                value, at = column(j, p, 256 - depth if s == 1 else depth - 1)
                to = 4 * g + p + VEL[j][0] + 1
                tile = jnp.where(lane_id == to, turn(value, to - at), tile)
        zs[side(s)] = tile
    tile = zero
    for s in (1, -1):
        for g, j in enumerate(LOCAL[s]):
            for p in (0, 1):
                value, at = column(j, p, 0 if s == 1 else 255)
                to = LOCAL_LANE[s] + 4 * g + p + VEL[j][0] + 1
                tile = jnp.where(lane_id == to, turn(value, to - at), tile)
    ls[0] = tile
    small = [m for m in MESSAGES if m[0] in ("z", "l")]
    small = sorted(small, key=lambda m: -sum(map(abs, m[1])))
    planes = [m for m in MESSAGES if m[0] in ("xb", "xa")]
    rows = sorted([m for m in MESSAGES if m[0] == "y"], key=lambda m: -abs(m[1][0]))
    for m in small + planes:
        send_when(m, earlier(m[1]))
    for s in (1, -1):
        for g, (j, depth) in enumerate(ROWS[s]):
            for p in (0, 1):
                row = 8 - depth if s == 1 else depth - 1
                ys[side(s), 2 * g + p : 2 * g + p + 1] = block[POS[j], 2 + p, row : row + 1]
    for m in rows:
        send_when(m, earlier(m[1]))

    def send_later(d):
        @pl.when(later(d))
        def _():
            pl.semaphore_wait(entered.at[DIRECTIONS.index(d)], 1)
            for m in small + planes + rows + [m for m in MESSAGES if m[0] == "xp"]:
                if m[1] == d:
                    copy_of(m).start()

    for d in DIRECTIONS:
        if upward(d):
            send_later(d)
    for d in DIRECTIONS:
        if max(d) < 1:
            send_later(d)

    for m in MESSAGES:
        @pl.when(has(opposite(m[1])))
        def _():
            copy_of(m).wait_recv()

    group_id = lane_id // 4
    lane_cx = jnp.where(group_id < 5, -1, jnp.where(group_id < 19, 0, 1))
    lane_cx = jnp.where(group_id >= 24, jnp.where(group_id < 25, -1, jnp.where(group_id < 28, 0, 1)), lane_cx)
    source = lane_id % 4 - 1 - lane_cx
    straight, shifted = {}, {}
    for s in (1, -1):
        merged = {}
        for dy in STEPS:
            parts = []
            for dx in STEPS:
                local = ls[0] if dx == 0 and dy == 0 else lr[dx + 1, dy + 1]
                if s == -1:
                    local = turn(local, 32)
                part = jnp.where(lane_id >= 96, local, zr[side(s), dx + 1, dy + 1])
                parts.append(turn(part, -2 * dx))
            merged[dy] = jnp.where(source < 0, parts[2], jnp.where(source > 1, parts[0], parts[1]))
        below, own, above = merged[1], merged[0], merged[-1]
        top, bottom = row_id == 0, row_id == 7
        straight[s, 0] = own
        straight[s, 1] = jnp.where(top, slide(below, 1), slide(own, 1))
        straight[s, -1] = jnp.where(bottom, slide(above, -1), slide(own, -1))
        shifted[s, 0] = jnp.where(top, slide(below, 1), slide(above, -1))
        shifted[s, 1] = jnp.where(top, slide(below, 2), own)
        shifted[s, -1] = jnp.where(bottom, slide(above, -2), own)

    def y_moved(value, sign, edge_row):
        edge = 0 if sign == 1 else 7
        return [jnp.where(row_id == edge, edge_row[h], slide(value[h], sign)) for h in (0, 1)]

    def z_moved(value, sign, edge_tile):
        rolled = [turn(v, sign) for v in value]
        if sign == 1:
            at = lane_id == 0
            return [jnp.where(at, edge_tile, rolled[0]), jnp.where(at, rolled[0], rolled[1])]
        at = lane_id == 127
        return [jnp.where(at, rolled[1], rolled[0]), jnp.where(at, edge_tile, rolled[1])]

    def edge_lane(sign):
        return 0 if sign == 1 else 127

    def incoming_row(s, j, depth, plane):
        p = plane - VEL[j][0]
        dx = 1 if p < 0 else -1 if p > 1 else 0
        k = 2 * ROWS[s].index((j, depth)) + p + 2 * dx
        return [yr[side(s), dx + 1, k : k + 1, lanes(h)] for h in (0, 1)]

    def presence(axis, sign):
        return exists[axis, sign].astype(jnp.float32)

    for plane in NEAR:
        for i in range(19):
            cx, cy, cz = VELOCITIES[i]
            value = [block[POS[i], plane - cx + 2, :, lanes(h)] for h in (0, 1)]
            if cy != 0:
                value = y_moved(value, cy, incoming_row(cy, i, 1, plane))
            if cz != 0:
                at = 4 * COLS[cz].index((i, 1)) + plane + 1
                value = z_moved(value, cz, turn(straight[cz, cy], edge_lane(cz) - at))
            for h in (0, 1):
                first[i, plane + 1, :, lanes(h)] = value[h]
        inside, wanted = None, range(19)
        if plane == -1:
            inside, wanted = one * presence(0, -1), [i for i in range(19) if VELOCITIES[i][0] == 1]
        if plane == 2:
            inside, wanted = one * presence(0, 1), [i for i in range(19) if VELOCITIES[i][0] == -1]
        for h in (0, 1):
            z = lanes(h)
            post = collide(
                [first[i, plane + 1, :, z] for i in range(19)],
                block[POS[KIND], plane + 2, :, z],
                block[POS[RELAX], plane + 2, :, z],
                [block[POS[INFLOW + a], plane + 2, :, z] for a in range(3)],
                wanted, inside,
            )
            for i in wanted:
                second[i, plane + 1, :, z] = post[i]

    lowest, highest = row_id % 4 == 0, row_id % 4 == 3
    beside = jnp.where(lowest, presence(0, -1), jnp.where(highest, presence(0, 1), one))
    outside = beside * jnp.where(row_id < 4, presence(1, -1), presence(1, 1))
    edges = {}
    for s in (1, -1):
        for cy in STEPS:
            tile = shifted[s, cy]
            tile = jnp.where(row_id < 4, tile[0:1], turn(jnp.broadcast_to(tile[7:8], (8, 128)), 4))
            aligned = tile
            for r in range(1, 8):
                aligned = jnp.where(row_id == r, turn(tile, -r), aligned)
            edges[s, cy] = aligned
    for j in FIELDS:
        cx, cy, cz = VEL[j]
        for s in (1, -1):
            for plane in NEAR:
                k = 4 * side(s) + plane + 1
                if cy == -s:
                    row = 0 if s == 1 else 7
                    row_tile[j, k : k + 1] = block[POS[j], plane - cx + 2, row : row + 1]
                else:
                    value = incoming_row(s, j, 1 if cy == 0 else 2, plane)
                    for h in (0, 1):
                        row_tile[j, k : k + 1, lanes(h)] = value[h]
    for i in range(19):
        cx, cy, cz = VELOCITIES[i]
        if cz != 0:
            value = [row_tile[i, :, lanes(h)] for h in (0, 1)]
            at = 4 * COLS[cz].index((i, 1))
            value = z_moved(value, cz, turn(edges[cz, cy], edge_lane(cz) - at))
            for h in (0, 1):
                row_tile[i, :, lanes(h)] = value[h]
    moving_y = [i for i in range(19) if VELOCITIES[i][1] != 0]
    for h in (0, 1):
        f = [row_tile[j, :, lanes(h)] for j in FIELDS]
        post = collide(f[:19], f[KIND], f[RELAX], f[INFLOW : INFLOW + 3], moving_y, outside)
        for i in moving_y:
            row_post[i, :, lanes(h)] = post[i]

    def column_tile(j):
        _, cy, cz = VEL[j]
        tile = None
        for s in (1, -1):
            if cz == -s:
                at = 96 + 4 * LOCAL[s].index(j)
            else:
                at = 4 * COLS[s].index((j, 1 if cz == 0 else 2))
            for outer, parts in ((0, straight), (8, shifted)):
                start = outer + 4 * side(s)
                part = turn(parts[s, cy], start - at)
                here = jnp.logical_and(lane_id >= start, lane_id < start + 4)
                tile = part if tile is None else jnp.where(here, part, tile)
        return tile

    lowest, highest = lane_id % 4 == 0, lane_id % 4 == 3
    beside = jnp.where(lowest, presence(0, -1), jnp.where(highest, presence(0, 1), one))
    outside = beside * jnp.where(lane_id % 8 < 4, presence(2, -1), presence(2, 1))
    beyond = jnp.where(row_id == 0, presence(1, -1), presence(1, 1))
    outside = outside * jnp.where(lane_id < 8, one, beyond)
    f = [column_tile(j) for j in FIELDS]
    moving_z = [i for i in range(19) if VELOCITIES[i][2] != 0]
    column_post = collide(f[:19], f[KIND], f[RELAX], f[INFLOW : INFLOW + 3], moving_z, outside)

    for p in (0, 1):
        acc = [[None, None] for _ in range(4)]
        for i in range(19):
            c = cx, cy, cz = VELOCITIES[i]
            plane = p - cx
            value = [second[i, plane + 1, :, lanes(h)] for h in (0, 1)]
            if cy != 0:
                k = 4 * side(cy) + plane + 1
                value = y_moved(value, cy, [row_post[i, k : k + 1, lanes(h)] for h in (0, 1)])
            if cz != 0:
                at = 4 * side(cz) + plane + 1
                edge = turn(column_post[i], edge_lane(cz) - at)
                if cy != 0:
                    corner = turn(column_post[i], edge_lane(cz) - at - 8)
                    edge = jnp.where(row_id == (0 if cy == 1 else 7), corner, slide(edge, cy))
                value = z_moved(value, cz, edge)
            for h in (0, 1):
                acc[0][h] = value[h] if acc[0][h] is None else acc[0][h] + value[h]
                for a in range(3):
                    if c[a] != 0:
                        old = zero if acc[1 + a][h] is None else acc[1 + a][h]
                        acc[1 + a][h] = old + value[h] if c[a] == 1 else old - value[h]
        for h in (0, 1):
            for k in range(4):
                out_ref[k, p, :, lanes(h)] = acc[k][h]

    for m in MESSAGES:
        @pl.when(has(m[1]))
        def _():
            copy_of(m).wait_send()


def finish(sums_ref, rho_hbm, mom_hbm, sems):
    copies = [
        pltpu.make_async_copy(sums_ref.at[0], rho_hbm, sems.at[0]),
        pltpu.make_async_copy(sums_ref.at[1:4], mom_hbm, sems.at[1]),
    ]
    for copy in copies:
        copy.start()
    for copy in copies:
        copy.wait()


def solution(mesh):
    sizes = tuple(mesh.shape[a] for a in AXES)
    count = len(MESSAGES)

    def shards(dist, site_kinds, relax, inflow):
        f32 = jnp.float32
        shape = site_kinds.shape
        sums = pl.pallas_call(
            functools.partial(kernel, sizes),
            out_shape=pltpu.VMEM((4,) + shape, f32),
            in_specs=[pl.BlockSpec(memory_space=pl.ANY)] * 4,
            out_specs=pl.BlockSpec(memory_space=pltpu.VMEM),
            scratch_shapes=[
                pltpu.VMEM((19,) + shape, f32),
                pltpu.VMEM(shape, jnp.int32),
                pltpu.VMEM((24, 6, 8, 256), f32),
                pltpu.VMEM((2, 48, 256), f32),
                pltpu.VMEM((2, 3, 48, 256), f32),
                pltpu.VMEM((2, 8, 128), f32),
                pltpu.VMEM((2, 3, 3, 8, 128), f32),
                pltpu.VMEM((1, 8, 128), f32),
                pltpu.VMEM((3, 3, 8, 128), f32),
                pltpu.VMEM((19, 4, 8, 256), f32),
                pltpu.VMEM((19, 4, 8, 256), f32),
                pltpu.VMEM((24, 8, 256), f32),
                pltpu.VMEM((19, 8, 256), f32),
                pltpu.SemaphoreType.DMA((2, 4)),
                pltpu.SemaphoreType.DMA((count,)),
                pltpu.SemaphoreType.DMA((count,)),
                pltpu.SemaphoreType.REGULAR((len(DIRECTIONS),)),
            ],
            compiler_params=pltpu.CompilerParams(collective_id=0, has_side_effects=True),
        )(dist, site_kinds, relax, inflow)
        return pl.pallas_call(
            finish,
            out_shape=(
                jax.ShapeDtypeStruct(shape, f32),
                jax.ShapeDtypeStruct((3,) + shape, f32),
            ),
            in_specs=[pl.BlockSpec(memory_space=pltpu.VMEM)],
            out_specs=(pl.BlockSpec(memory_space=pl.ANY), pl.BlockSpec(memory_space=pl.ANY)),
            scratch_shapes=[pltpu.SemaphoreType.DMA((2,))],
        )(pltpu.with_memory_space_constraint(sums, pltpu.VMEM))

    return jax.shard_map(
        shards,
        mesh=mesh,
        in_specs=(
            P(None, "gx", "gy", "gz"),
            P("gx", "gy", "gz"),
            P("gx", "gy", "gz"),
            P(None, "gx", "gy", "gz"),
        ),
        out_specs=(P("gx", "gy", "gz"), P(None, "gx", "gy", "gz")),
        check_vma=False,
    )
```

time: 70.1 us -> 21.5 us (0.31)
  the two profiles are of different devices: /device:TPU:346 before, /device:TPU:65 now
where the time goes in v3:
time: 21.5 us; the launch traced here: 21.3 us
  Pallas kernels  20.7 us (96%)
  between operations  0.64 us (3%)
    pallas_call x1, Pallas kernels, shards(): pl.pallas_call(functools.partial(kernel, sizes), out_shape=pltpu.VMEM((4,...  20.1 us
    pallas_call x1, Pallas kernels, shards(): pl.pallas_call(finish, out_shape=(jax.ShapeDtypeStruct(shape, f32), jax.S...  0.65 us

profile of v3, /device:TPU:65, one launch (start us, length us, event | category | flops | bytes accessed | tf_op | source)
XLA Modules:
  0.0 21.3 jit_solution(3077134114520162752)
XLA Ops:
  0.6 20.1 %shard_map.59.sums_ref = f32[4,2,8,256]{3,2,1,0:T(8,128)S(1)} custom-call(f32[19,2,8,256]{3,2,1,0:T(8,128)} %dist_hbm.1, s32[2,8,256]{2,1,0:T(8,128)} %kinds_hbm.1, f32[2,8,256]{2,1,0:T(8,128)} %relax_hbm.1, f32[3,2,8,256]{3,2,1,0:T(8,128)} %inflow_hbm.1), custom_call_target="tpu_custom_call" | custom-call | tf_op jit(solution)/shard_map/pallas_call | solution.py:507
  20.7 0.6 %shard_map.60 = (f32[2,8,256]{2,1,0:T(8,128)}, f32[3,2,8,256]{3,2,1,0:T(8,128)}) custom-call(f32[4,2,8,256]{3,2,1,0:T(8,128)S(1)} %shard_map.59.sums_ref), custom_call_target="tpu_custom_call" | custom-call | tf_op jit(solution)/shard_map/pallas_call | solution.py:533

commit v4 on v3

--- a/solution.py
+++ b/solution.py
@@ -1,4 +1,5 @@
 import functools
+import itertools
 
 import jax
 import jax.numpy as jnp
@@ -66,6 +67,14 @@
     return next(s for s in (d[0], d[2], d[1]) if s != 0) == 1
 
 
+def row_place(g, p):
+    if g < 5:
+        return 2 * g + p
+    if g < 19:
+        return 10 + 14 * p + g - 5
+    return 38 + 2 * (g - 19) + p
+
+
 def messages():
     found = []
     for d in DIRECTIONS:
@@ -84,10 +93,16 @@
 MESSAGES = messages()
 
 
+def tiles(m):
+    if m[0] == "y":
+        return 12 if m[1][0] == 0 else 6
+    return {"xp": 10, "xb": 18, "xa": 20, "z": 1, "l": 1}[m[0]]
+
+
 def kernel(
     sizes, dist_hbm, kinds_hbm, relax_hbm, inflow_hbm, out_ref,
     field, kinds, block, ys, yr, zs, zr, ls, lr, first, second, row_tile, row_post,
-    load_sem, send_sem, recv_sem, entered,
+    size_ref, load_sem, send_sem, recv_sem, entered,
 ):
     me = tuple(lax.axis_index(a) for a in AXES)
     exists = {}
@@ -102,19 +117,17 @@
     def target(direction):
         return tuple(m + s for m, s in zip(me, direction))
 
-    loads = []
     for p in (1, 0):
         group = [
-            pltpu.make_async_copy(kinds_hbm.at[p], kinds.at[p], load_sem.at[p, 0]),
-            pltpu.make_async_copy(relax_hbm.at[p], block.at[POS[RELAX], 2 + p], load_sem.at[p, 1]),
+            pltpu.make_async_copy(kinds_hbm.at[p], kinds.at[p], load_sem.at[p]),
+            pltpu.make_async_copy(relax_hbm.at[p], block.at[POS[RELAX], 2 + p], load_sem.at[p]),
             pltpu.make_async_copy(
-                inflow_hbm.at[:, p], block.at[POS[INFLOW] : POS[INFLOW] + 3, 2 + p], load_sem.at[p, 2]
+                inflow_hbm.at[:, p], block.at[POS[INFLOW] : POS[INFLOW] + 3, 2 + p], load_sem.at[p]
             ),
-            pltpu.make_async_copy(dist_hbm.at[:, p], field.at[:, p], load_sem.at[p, 3]),
+            pltpu.make_async_copy(dist_hbm.at[:, p], field.at[:, p], load_sem.at[p]),
         ]
         for copy in group:
             copy.start()
-        loads.append(group)
 
     def is_origin(place):
         return jnp.logical_and(place[0] == 0, jnp.logical_and(place[1] == 0, place[2] == 0))
@@ -155,7 +168,7 @@
             mine, theirs = (3, 1) if dx == 1 else (2, 4)
             return block.at[at, mine : mine + 1], block.at[at, theirs : theirs + 1]
         if kind == "y":
-            rows = {0: slice(0, 48), 1: slice(8, 48), -1: slice(0, 40)}[dx]
+            rows = {0: slice(0, 48), 1: slice(24, 48), -1: slice(0, 24)}[dx]
             return ys.at[side(dy), rows], yr.at[side(dy), dx + 1, rows]
         if kind == "z":
             return zs.at[side(dz)], zr.at[side(dz), dx + 1, dy + 1]
@@ -163,11 +176,27 @@
 
     def copy_of(m):
         src, dst = ends(m)
-        k = MESSAGES.index(m)
         return pltpu.make_async_remote_copy(
-            src_ref=src, dst_ref=dst, send_sem=send_sem.at[k], recv_sem=recv_sem.at[k],
+            src_ref=src, dst_ref=dst, send_sem=send_sem.at[0], recv_sem=recv_sem.at[side(m[1][0])],
             device_id=target(m[1]), device_id_type=MESH,
         )
+
+    def await_tiles(count, sem):
+        part = size_ref.at[0:count]
+        pltpu.make_async_copy(part, part, sem).wait()
+
+    def await_present(found, toward, sem):
+        count = 0
+        for m in found:
+            count = count + tiles(m) * has(toward(m[1])).astype(jnp.int32)
+        sums = set()
+        for touched in itertools.product(((), (1,), (-1,), (1, -1)), repeat=3):
+            known = [m for m in found if not any(v in touched[a] for a, v in enumerate(toward(m[1])))]
+            sums.add(sum(map(tiles, known)))
+        for total in sorted(sums - {0}):
+            @pl.when(count == total)
+            def _():
+                await_tiles(total, sem)
 
     for m in MESSAGES:
         @pl.when(jnp.logical_not(has(opposite(m[1]))))
@@ -226,29 +255,51 @@
                 post[i + 1] = keep * jnp.where(wall, f[i], f[i + 1]) + take * (even - odd)
         return post
 
-    def send_when(m, condition):
-        @pl.when(condition)
-        def _():
+    small = [m for m in MESSAGES if m[0] in ("z", "l")]
+    small = sorted(small, key=lambda m: -sum(map(abs, m[1])))
+    rows = sorted([m for m in MESSAGES if m[0] == "y"], key=lambda m: -abs(m[1][0]))
+    everything = small + [m for m in MESSAGES if m[0] in ("xp", "xb", "xa")] + rows
+
+    def start(found):
+        for m in found:
             copy_of(m).start()
+
+    def origin_starts(found):
+        there = [m for m in found if min(m[1]) >= 0 and all(sizes[a] > 1 for a in range(3) if m[1][a] == 1)]
+        if there:
+            @pl.when(here_origin)
+            def _():
+                start(there)
+
+    def all_to(d):
+        start([m for m in everything if m[1] == d])
 
     @pl.when(before > 0)
     def _():
         pl.semaphore_wait(barrier, before)
 
-    for d in DIRECTIONS:
-        @pl.when(earlier(d))
-        def _():
-            at = entered.at[DIRECTIONS.index(opposite(d))]
-            pl.semaphore_signal(at, inc=1, device_id=target(d), device_id_type=MESH)
-
-    for p, group in zip((1, 0), loads):
-        for copy in group[:3]:
-            copy.wait()
+    def answer(d, which):
+        pl.semaphore_signal(entered.at[which], inc=1, device_id=target(d), device_id_type=MESH)
+
+    @pl.when(here_origin)
+    def _():
+        for d in DIRECTIONS:
+            if min(d) >= 0 and all(sizes[a] > 1 for a in range(3) if d[a] == 1):
+                answer(d, 1)
+
+    @pl.when(jnp.logical_not(here_origin))
+    def _():
+        for d in DIRECTIONS:
+            if not upward(d):
+                @pl.when(earlier(d))
+                def _():
+                    answer(d, 0)
+
+    for p in (1, 0):
+        await_tiles(48, load_sem.at[p])
         block[POS[KIND], 2 + p] = kinds[p].astype(jnp.float32)
-        for m in MESSAGES:
-            if m[0] == "xp" and m[1][0] == (1 if p == 1 else -1):
-                send_when(m, earlier(m[1]))
-        group[3].wait()
+        if p == 1:
+            origin_starts([("xp", (1, 0, 0))])
         for h in (0, 1):
             z = lanes(h)
             post = collide(
@@ -260,6 +311,8 @@
             )
             for i in range(19):
                 block[POS[i], 2 + p, :, z] = post[i]
+        if p == 1:
+            origin_starts([("xb", (1, 0, 0))])
 
     def column(j, p, at):
         return block[POS[j], 2 + p, :, lanes(at // 128)], at % 128
@@ -280,64 +333,74 @@
                 to = LOCAL_LANE[s] + 4 * g + p + VEL[j][0] + 1
                 tile = jnp.where(lane_id == to, turn(value, to - at), tile)
     ls[0] = tile
-    small = [m for m in MESSAGES if m[0] in ("z", "l")]
-    small = sorted(small, key=lambda m: -sum(map(abs, m[1])))
-    planes = [m for m in MESSAGES if m[0] in ("xb", "xa")]
-    rows = sorted([m for m in MESSAGES if m[0] == "y"], key=lambda m: -abs(m[1][0]))
-    for m in small + planes:
-        send_when(m, earlier(m[1]))
+    origin_starts(small + [("xa", (1, 0, 0))])
     for s in (1, -1):
         for g, (j, depth) in enumerate(ROWS[s]):
             for p in (0, 1):
                 row = 8 - depth if s == 1 else depth - 1
-                ys[side(s), 2 * g + p : 2 * g + p + 1] = block[POS[j], 2 + p, row : row + 1]
-    for m in rows:
-        send_when(m, earlier(m[1]))
-
-    def send_later(d):
-        @pl.when(later(d))
-        def _():
-            pl.semaphore_wait(entered.at[DIRECTIONS.index(d)], 1)
-            for m in small + planes + rows + [m for m in MESSAGES if m[0] == "xp"]:
-                if m[1] == d:
-                    copy_of(m).start()
-
+                k = row_place(g, p)
+                ys[side(s), k : k + 1] = block[POS[j], 2 + p, row : row + 1]
+    origin_starts(rows)
+
+    after = 0
     for d in DIRECTIONS:
         if upward(d):
-            send_later(d)
-    for d in DIRECTIONS:
-        if max(d) < 1:
-            send_later(d)
-
-    for m in MESSAGES:
-        @pl.when(has(opposite(m[1])))
+            after = after + later(d).astype(jnp.int32)
+
+    @pl.when(jnp.logical_not(here_origin))
+    def _():
+        for d in DIRECTIONS:
+            if not upward(d):
+                @pl.when(earlier(d))
+                def _():
+                    all_to(d)
+
+        @pl.when(after > 0)
         def _():
-            copy_of(m).wait_recv()
+            pl.semaphore_wait(entered.at[0], after)
+
+        for d in DIRECTIONS:
+            if upward(d):
+                @pl.when(later(d))
+                def _():
+                    all_to(d)
+        for d in DIRECTIONS:
+            if max(d) < 1:
+                @pl.when(later(d))
+                def _():
+                    pl.semaphore_wait(entered.at[1], 1)
+                    all_to(d)
+
+    await_present([m for m in MESSAGES if m[1][0] != 1], opposite, recv_sem.at[1])
 
     group_id = lane_id // 4
     lane_cx = jnp.where(group_id < 5, -1, jnp.where(group_id < 19, 0, 1))
     lane_cx = jnp.where(group_id >= 24, jnp.where(group_id < 25, -1, jnp.where(group_id < 28, 0, 1)), lane_cx)
     source = lane_id % 4 - 1 - lane_cx
-    straight, shifted = {}, {}
-    for s in (1, -1):
-        merged = {}
-        for dy in STEPS:
-            parts = []
-            for dx in STEPS:
-                local = ls[0] if dx == 0 and dy == 0 else lr[dx + 1, dy + 1]
-                if s == -1:
-                    local = turn(local, 32)
-                part = jnp.where(lane_id >= 96, local, zr[side(s), dx + 1, dy + 1])
-                parts.append(turn(part, -2 * dx))
-            merged[dy] = jnp.where(source < 0, parts[2], jnp.where(source > 1, parts[0], parts[1]))
-        below, own, above = merged[1], merged[0], merged[-1]
-        top, bottom = row_id == 0, row_id == 7
-        straight[s, 0] = own
-        straight[s, 1] = jnp.where(top, slide(below, 1), slide(own, 1))
-        straight[s, -1] = jnp.where(bottom, slide(above, -1), slide(own, -1))
-        shifted[s, 0] = jnp.where(top, slide(below, 1), slide(above, -1))
-        shifted[s, 1] = jnp.where(top, slide(below, 2), own)
-        shifted[s, -1] = jnp.where(bottom, slide(above, -2), own)
+
+    def merge(steps_x):
+        straight, shifted = {}, {}
+        for s in (1, -1):
+            merged = {}
+            for dy in STEPS:
+                parts = {}
+                for dx in steps_x:
+                    local = ls[0] if dx == 0 and dy == 0 else lr[dx + 1, dy + 1]
+                    if s == -1:
+                        local = turn(local, 32)
+                    part = jnp.where(lane_id >= 96, local, zr[side(s), dx + 1, dy + 1])
+                    parts[dx] = turn(part, -2 * dx)
+                whole = jnp.where(source > 1, parts[-1], parts[0])
+                merged[dy] = jnp.where(source < 0, parts[1], whole) if 1 in parts else whole
+            below, own, above = merged[1], merged[0], merged[-1]
+            top, bottom = row_id == 0, row_id == 7
+            straight[s, 0] = own
+            straight[s, 1] = jnp.where(top, slide(below, 1), slide(own, 1))
+            straight[s, -1] = jnp.where(bottom, slide(above, -1), slide(own, -1))
+            shifted[s, 0] = jnp.where(top, slide(below, 1), slide(above, -1))
+            shifted[s, 1] = jnp.where(top, slide(below, 2), own)
+            shifted[s, -1] = jnp.where(bottom, slide(above, -2), own)
+        return straight, shifted
 
     def y_moved(value, sign, edge_row):
         edge = 0 if sign == 1 else 7
@@ -357,13 +420,13 @@
     def incoming_row(s, j, depth, plane):
         p = plane - VEL[j][0]
         dx = 1 if p < 0 else -1 if p > 1 else 0
-        k = 2 * ROWS[s].index((j, depth)) + p + 2 * dx
+        k = row_place(ROWS[s].index((j, depth)), p + 2 * dx)
         return [yr[side(s), dx + 1, k : k + 1, lanes(h)] for h in (0, 1)]
 
     def presence(axis, sign):
         return exists[axis, sign].astype(jnp.float32)
 
-    for plane in NEAR:
+    def collide_plane(plane, straight):
         for i in range(19):
             cx, cy, cz = VELOCITIES[i]
             value = [block[POS[i], plane - cx + 2, :, lanes(h)] for h in (0, 1)]
@@ -390,6 +453,14 @@
             )
             for i in wanted:
                 second[i, plane + 1, :, z] = post[i]
+
+    partial, _ = merge((-1, 0))
+    for plane in (1, 2):
+        collide_plane(plane, partial)
+    await_present([m for m in MESSAGES if m[1][0] == 1], opposite, recv_sem.at[0])
+    straight, shifted = merge(STEPS)
+    for plane in (-1, 0):
+        collide_plane(plane, straight)
 
     lowest, highest = row_id % 4 == 0, row_id % 4 == 3
     beside = jnp.where(lowest, presence(0, -1), jnp.where(highest, presence(0, 1), one))
@@ -480,10 +551,7 @@
             for k in range(4):
                 out_ref[k, p, :, lanes(h)] = acc[k][h]
 
-    for m in MESSAGES:
-        @pl.when(has(m[1]))
-        def _():
-            copy_of(m).wait_send()
+    await_present(MESSAGES, lambda d: d, send_sem.at[0])
 
 
 def finish(sums_ref, rho_hbm, mom_hbm, sems):
@@ -499,7 +567,6 @@
 
 def solution(mesh):
     sizes = tuple(mesh.shape[a] for a in AXES)
-    count = len(MESSAGES)
 
     def shards(dist, site_kinds, relax, inflow):
         f32 = jnp.float32
@@ -523,10 +590,11 @@
                 pltpu.VMEM((19, 4, 8, 256), f32),
                 pltpu.VMEM((24, 8, 256), f32),
                 pltpu.VMEM((19, 8, 256), f32),
-                pltpu.SemaphoreType.DMA((2, 4)),
-                pltpu.SemaphoreType.DMA((count,)),
-                pltpu.SemaphoreType.DMA((count,)),
-                pltpu.SemaphoreType.REGULAR((len(DIRECTIONS),)),
+                pltpu.VMEM((sum(map(tiles, MESSAGES)), 8, 128), f32),
+                pltpu.SemaphoreType.DMA((2,)),
+                pltpu.SemaphoreType.DMA((1,)),
+                pltpu.SemaphoreType.DMA((2,)),
+                pltpu.SemaphoreType.REGULAR((2,)),
             ],
             compiler_params=pltpu.CompilerParams(collective_id=0, has_side_effects=True),
         )(dist, site_kinds, relax, inflow)

time: 21.5 us -> 20.2 us (0.940)
  Pallas kernels: 20.7 us -> 19.4 us
    pallas_call x1, Pallas kernels: 20.1 us -> 18.7 us  [shards(): pl.pallas_call(functools.partial(kernel, sizes), out_shape=pltpu.VMEM((4,...]
where the time goes in v4:
time: 20.2 us; the launch traced here: 20 us
  Pallas kernels  19.4 us (96%)
  between operations  0.64 us (3%)
    pallas_call x1, Pallas kernels, shards(): pl.pallas_call(functools.partial(kernel, sizes), out_shape=pltpu.VMEM((4,...  18.7 us
    pallas_call x1, Pallas kernels, shards(): pl.pallas_call(finish, out_shape=(jax.ShapeDtypeStruct(shape, f32), jax.S...  0.65 us

profile of v4, /device:TPU:65, one launch (start us, length us, event | category | flops | bytes accessed | tf_op | source)
XLA Modules:
  0.0 20.0 jit_solution(17329693601297643047)
XLA Ops:
  0.6 18.7 %shard_map.59.sums_ref = f32[4,2,8,256]{3,2,1,0:T(8,128)S(1)} custom-call(f32[19,2,8,256]{3,2,1,0:T(8,128)} %dist_hbm.1, s32[2,8,256]{2,1,0:T(8,128)} %kinds_hbm.1, f32[2,8,256]{2,1,0:T(8,128)} %relax_hbm.1, f32[3,2,8,256]{3,2,1,0:T(8,128)} %inflow_hbm.1), custom_call_target="tpu_custom_call" | custom-call | tf_op jit(solution)/shard_map/pallas_call | solution.py:574
  19.4 0.6 %shard_map.60 = (f32[2,8,256]{2,1,0:T(8,128)}, f32[3,2,8,256]{3,2,1,0:T(8,128)}) custom-call(f32[4,2,8,256]{3,2,1,0:T(8,128)S(1)} %shard_map.59.sums_ref), custom_call_target="tpu_custom_call" | custom-call | tf_op jit(solution)/shard_map/pallas_call | solution.py:601

commit v5 on v4

--- a/solution.py
+++ b/solution.py
@@ -53,6 +53,8 @@
 COLS = {s: groups(2, s) for s in (1, -1)}
 LOCAL = {s: sorted([j for j in FIELDS if VEL[j][2] == -s], key=lambda j: VEL[j][0]) for s in (1, -1)}
 LOCAL_LANE = {1: 96, -1: 64}
+LEVEL = [i for i in range(19) if VELOCITIES[i][0] == 0]
+FACE_ROWS = {s: [i for i in LEVEL if VELOCITIES[i][1] == -s] for s in (1, -1)}
 
 
 def side(sign):
@@ -80,7 +82,7 @@
     for d in DIRECTIONS:
         dx, dy, dz = d
         if dy == 0 and dz == 0:
-            found += [("xp", d), ("xb", d), ("xa", d)]
+            found += [("xp", d), ("xs", d), ("xa", d)]
         if dz == 0 and dy != 0:
             found.append(("y", d))
         if dz != 0:
@@ -96,12 +98,12 @@
 def tiles(m):
     if m[0] == "y":
         return 12 if m[1][0] == 0 else 6
-    return {"xp": 10, "xb": 18, "xa": 20, "z": 1, "l": 1}[m[0]]
+    return {"xp": 10, "xs": 8, "xa": 20, "z": 1, "l": 1}[m[0]]
 
 
 def kernel(
     sizes, dist_hbm, kinds_hbm, relax_hbm, inflow_hbm, out_ref,
-    field, kinds, block, ys, yr, zs, zr, ls, lr, first, second, row_tile, row_post,
+    field, kinds, block, xs, xr, ys, yr, zs, zr, ls, lr, first, second, row_tile, row_post,
     size_ref, load_sem, send_sem, recv_sem, entered,
 ):
     me = tuple(lax.axis_index(a) for a in AXES)
@@ -163,10 +165,11 @@
         if kind == "xa":
             at, mine, theirs = (slice(0, 5), slice(2, 4), slice(0, 2)) if dx == 1 else (slice(19, 24), slice(2, 4), slice(4, 6))
             return block.at[at, mine], block.at[at, theirs]
-        if kind in ("xb", "xp"):
-            at = slice(5, 14) if kind == "xb" else slice(14, 19)
+        if kind == "xp":
             mine, theirs = (3, 1) if dx == 1 else (2, 4)
-            return block.at[at, mine : mine + 1], block.at[at, theirs : theirs + 1]
+            return block.at[14:19, mine : mine + 1], block.at[14:19, theirs : theirs + 1]
+        if kind == "xs":
+            return xs.at[side(dx)], xr.at[side(dx)]
         if kind == "y":
             rows = {0: slice(0, 48), 1: slice(24, 48), -1: slice(0, 24)}[dx]
             return ys.at[side(dy), rows], yr.at[side(dy), dx + 1, rows]
@@ -219,13 +222,31 @@
     def lanes(h):
         return slice(h * 128, h * 128 + 128)
 
-    def collide(f, kind, relax, inflow, wanted, inside=None):
-        rho = functools.reduce(jnp.add, f)
+    def y_moved(value, sign, edge_row):
+        edge = 0 if sign == 1 else 7
+        return [jnp.where(row_id == edge, edge_row[h], slide(value[h], sign)) for h in (0, 1)]
+
+    def z_moved(value, sign, edge_tile):
+        rolled = [turn(v, sign) for v in value]
+        if sign == 1:
+            at = lane_id == 0
+            return [jnp.where(at, edge_tile, rolled[0]), jnp.where(at, rolled[0], rolled[1])]
+        at = lane_id == 127
+        return [jnp.where(at, rolled[1], rolled[0]), jnp.where(at, edge_tile, rolled[1])]
+
+    def edge_lane(sign):
+        return 0 if sign == 1 else 127
+
+    def collide(f, kind, relax, inflow, wanted, inside=None, level=None):
+        present = [i for i in range(19) if f[i] is not None]
+        rho = functools.reduce(jnp.add, [f[i] for i in present])
         u = []
         for axis in range(3):
-            plus = [f[i] for i in range(19) if VELOCITIES[i][axis] == 1]
-            minus = [f[i] for i in range(19) if VELOCITIES[i][axis] == -1]
+            plus = [f[i] for i in present if VELOCITIES[i][axis] == 1]
+            minus = [f[i] for i in present if VELOCITIES[i][axis] == -1]
             u.append(functools.reduce(jnp.add, plus) - functools.reduce(jnp.add, minus))
+        if level is not None:
+            rho, u = rho + level[0], [u[0], u[1] + level[1], u[2] + level[2]]
         wall, fluid = kind < 0.5, jnp.logical_and(kind > 0.5, kind < 1.5)
         inlet, outlet = jnp.logical_and(kind > 1.5, kind < 2.5), kind > 2.5
         r = jnp.where(outlet, one, rho)
@@ -258,7 +279,7 @@
     small = [m for m in MESSAGES if m[0] in ("z", "l")]
     small = sorted(small, key=lambda m: -sum(map(abs, m[1])))
     rows = sorted([m for m in MESSAGES if m[0] == "y"], key=lambda m: -abs(m[1][0]))
-    everything = small + [m for m in MESSAGES if m[0] in ("xp", "xb", "xa")] + rows
+    everything = small + [m for m in MESSAGES if m[0] in ("xp", "xs", "xa")] + rows
 
     def start(found):
         for m in found:
@@ -273,6 +294,32 @@
 
     def all_to(d):
         start([m for m in everything if m[1] == d])
+
+    def add_level(sums, i, value):
+        for n, factor in enumerate((1, VELOCITIES[i][1], VELOCITIES[i][2])):
+            for h in (0, 1):
+                if factor != 0:
+                    sums[n][h] = sums[n][h] + value[h] if factor == 1 else sums[n][h] - value[h]
+
+    def sum_level(dx):
+        p = 1 if dx == 1 else 0
+        sums = [[zero, zero] for _ in range(3)]
+        for i in LEVEL:
+            _, cy, cz = VELOCITIES[i]
+            value = [block[POS[i], 2 + p, :, lanes(h)] for h in (0, 1)]
+            if cy != 0:
+                value = y_moved(value, cy, [zero, zero])
+            if cz != 0:
+                value = z_moved(value, cz, zero)
+            add_level(sums, i, value)
+        for h in (0, 1):
+            for n in range(3):
+                xs[side(dx), n, :, lanes(h)] = sums[n][h]
+            xs[side(dx), 3, :, lanes(h)] = zero
+        for s in (1, -1):
+            for n, j in enumerate(FACE_ROWS[s]):
+                k, row = 3 * side(s) + n, 0 if s == 1 else 7
+                xs[side(dx), 3, k : k + 1] = block[POS[j], 2 + p, row : row + 1]
 
     @pl.when(before > 0)
     def _():
@@ -312,7 +359,16 @@
             for i in range(19):
                 block[POS[i], 2 + p, :, z] = post[i]
         if p == 1:
-            origin_starts([("xb", (1, 0, 0))])
+            sum_level(1)
+            origin_starts([("xs", (1, 0, 0))])
+
+    for s in (1, -1):
+        for g, (j, depth) in enumerate(ROWS[s]):
+            for p in (0, 1):
+                row = 8 - depth if s == 1 else depth - 1
+                k = row_place(g, p)
+                ys[side(s), k : k + 1] = block[POS[j], 2 + p, row : row + 1]
+    origin_starts([("y", (0, 1, 0))])
 
     def column(j, p, at):
         return block[POS[j], 2 + p, :, lanes(at // 128)], at % 128
@@ -334,13 +390,8 @@
                 tile = jnp.where(lane_id == to, turn(value, to - at), tile)
     ls[0] = tile
     origin_starts(small + [("xa", (1, 0, 0))])
-    for s in (1, -1):
-        for g, (j, depth) in enumerate(ROWS[s]):
-            for p in (0, 1):
-                row = 8 - depth if s == 1 else depth - 1
-                k = row_place(g, p)
-                ys[side(s), k : k + 1] = block[POS[j], 2 + p, row : row + 1]
-    origin_starts(rows)
+    origin_starts([m for m in rows if m[1] != (0, 1, 0)])
+    sum_level(-1)
 
     after = 0
     for d in DIRECTIONS:
@@ -402,21 +453,6 @@
             shifted[s, -1] = jnp.where(bottom, slide(above, -2), own)
         return straight, shifted
 
-    def y_moved(value, sign, edge_row):
-        edge = 0 if sign == 1 else 7
-        return [jnp.where(row_id == edge, edge_row[h], slide(value[h], sign)) for h in (0, 1)]
-
-    def z_moved(value, sign, edge_tile):
-        rolled = [turn(v, sign) for v in value]
-        if sign == 1:
-            at = lane_id == 0
-            return [jnp.where(at, edge_tile, rolled[0]), jnp.where(at, rolled[0], rolled[1])]
-        at = lane_id == 127
-        return [jnp.where(at, rolled[1], rolled[0]), jnp.where(at, edge_tile, rolled[1])]
-
-    def edge_lane(sign):
-        return 0 if sign == 1 else 127
-
     def incoming_row(s, j, depth, plane):
         p = plane - VEL[j][0]
         dx = 1 if p < 0 else -1 if p > 1 else 0
@@ -427,14 +463,25 @@
         return exists[axis, sign].astype(jnp.float32)
 
     def collide_plane(plane, straight):
+        near = plane in (-1, 2)
+        sums = None
+        if near:
+            ends_at = 0 if plane == -1 else 1
+            sums = [[xr[ends_at, n, :, lanes(h)] for h in (0, 1)] for n in range(3)]
         for i in range(19):
             cx, cy, cz = VELOCITIES[i]
-            value = [block[POS[i], plane - cx + 2, :, lanes(h)] for h in (0, 1)]
+            if near and cx == 0:
+                value = [zero, zero]
+            else:
+                value = [block[POS[i], plane - cx + 2, :, lanes(h)] for h in (0, 1)]
             if cy != 0:
                 value = y_moved(value, cy, incoming_row(cy, i, 1, plane))
             if cz != 0:
                 at = 4 * COLS[cz].index((i, 1)) + plane + 1
                 value = z_moved(value, cz, turn(straight[cz, cy], edge_lane(cz) - at))
+            if near and cx == 0:
+                add_level(sums, i, value)
+                continue
             for h in (0, 1):
                 first[i, plane + 1, :, lanes(h)] = value[h]
         inside, wanted = None, range(19)
@@ -445,19 +492,40 @@
         for h in (0, 1):
             z = lanes(h)
             post = collide(
-                [first[i, plane + 1, :, z] for i in range(19)],
+                [None if near and i in LEVEL else first[i, plane + 1, :, z] for i in range(19)],
                 block[POS[KIND], plane + 2, :, z],
                 block[POS[RELAX], plane + 2, :, z],
                 [block[POS[INFLOW + a], plane + 2, :, z] for a in range(3)],
-                wanted, inside,
+                wanted, inside, [sums[n][h] for n in range(3)] if near else None,
             )
             for i in wanted:
                 second[i, plane + 1, :, z] = post[i]
 
+    def fill_rows(from_below):
+        for j in FIELDS:
+            cx, cy, cz = VEL[j]
+            for s in (1, -1):
+                for plane in NEAR:
+                    if (plane - cx < 0) != from_below:
+                        continue
+                    k = 4 * side(s) + plane + 1
+                    if cy == -s and cx == 0 and plane in (-1, 2):
+                        n = 3 * side(s) + FACE_ROWS[s].index(j)
+                        row_tile[j, k : k + 1] = xr[0 if plane == -1 else 1, 3, n : n + 1]
+                    elif cy == -s:
+                        row = 0 if s == 1 else 7
+                        row_tile[j, k : k + 1] = block[POS[j], plane - cx + 2, row : row + 1]
+                    else:
+                        value = incoming_row(s, j, 1 if cy == 0 else 2, plane)
+                        for h in (0, 1):
+                            row_tile[j, k : k + 1, lanes(h)] = value[h]
+
     partial, _ = merge((-1, 0))
+    fill_rows(False)
     for plane in (1, 2):
         collide_plane(plane, partial)
     await_present([m for m in MESSAGES if m[1][0] == 1], opposite, recv_sem.at[0])
+    fill_rows(True)
     straight, shifted = merge(STEPS)
     for plane in (-1, 0):
         collide_plane(plane, straight)
@@ -474,18 +542,6 @@
             for r in range(1, 8):
                 aligned = jnp.where(row_id == r, turn(tile, -r), aligned)
             edges[s, cy] = aligned
-    for j in FIELDS:
-        cx, cy, cz = VEL[j]
-        for s in (1, -1):
-            for plane in NEAR:
-                k = 4 * side(s) + plane + 1
-                if cy == -s:
-                    row = 0 if s == 1 else 7
-                    row_tile[j, k : k + 1] = block[POS[j], plane - cx + 2, row : row + 1]
-                else:
-                    value = incoming_row(s, j, 1 if cy == 0 else 2, plane)
-                    for h in (0, 1):
-                        row_tile[j, k : k + 1, lanes(h)] = value[h]
     for i in range(19):
         cx, cy, cz = VELOCITIES[i]
         if cz != 0:
@@ -580,6 +636,8 @@
                 pltpu.VMEM((19,) + shape, f32),
                 pltpu.VMEM(shape, jnp.int32),
                 pltpu.VMEM((24, 6, 8, 256), f32),
+                pltpu.VMEM((2, 4, 8, 256), f32),
+                pltpu.VMEM((2, 4, 8, 256), f32),
                 pltpu.VMEM((2, 48, 256), f32),
                 pltpu.VMEM((2, 3, 48, 256), f32),
                 pltpu.VMEM((2, 8, 128), f32),

time: 20.2 us -> 19.7 us (0.975)
  Pallas kernels: 19.4 us -> 18.9 us
    pallas_call x1, Pallas kernels: 18.7 us -> 18.3 us  [shards(): pl.pallas_call(functools.partial(kernel, sizes), out_shape=pltpu.VMEM((4,...]
where the time goes in v5:
time: 19.7 us; the launch traced here: 19.6 us
  Pallas kernels  18.9 us (96%)
  between operations  0.64 us (3%)
    pallas_call x1, Pallas kernels, shards(): pl.pallas_call(functools.partial(kernel, sizes), out_shape=pltpu.VMEM((4,...  18.3 us
    pallas_call x1, Pallas kernels, shards(): pl.pallas_call(finish, out_shape=(jax.ShapeDtypeStruct(shape, f32), jax.S...  0.65 us

profile of v5, /device:TPU:65, one launch (start us, length us, event | category | flops | bytes accessed | tf_op | source)
XLA Modules:
  0.0 19.6 jit_solution(8840160890430118841)
XLA Ops:
  0.6 18.3 %shard_map.59.sums_ref = f32[4,2,8,256]{3,2,1,0:T(8,128)S(1)} custom-call(f32[19,2,8,256]{3,2,1,0:T(8,128)} %dist_hbm.1, s32[2,8,256]{2,1,0:T(8,128)} %kinds_hbm.1, f32[2,8,256]{2,1,0:T(8,128)} %relax_hbm.1, f32[3,2,8,256]{3,2,1,0:T(8,128)} %inflow_hbm.1), custom_call_target="tpu_custom_call" | custom-call | tf_op jit(solution)/shard_map/pallas_call | solution.py:630
  18.9 0.6 %shard_map.60 = (f32[2,8,256]{2,1,0:T(8,128)}, f32[3,2,8,256]{3,2,1,0:T(8,128)}) custom-call(f32[4,2,8,256]{3,2,1,0:T(8,128)S(1)} %shard_map.59.sums_ref), custom_call_target="tpu_custom_call" | custom-call | tf_op jit(solution)/shard_map/pallas_call | solution.py:659

commit v6 on v5

--- a/solution.py
+++ b/solution.py
@@ -33,9 +33,9 @@
 AXES = ("gx", "gy", "gz")
 MESH = pl.DeviceIdType.MESH
 
-KIND, RELAX, INFLOW = 19, 20, 21
-VEL = VELOCITIES + [(0, 0, 0)] * 5
-FIELDS = range(24)
+KIND, OWN, INFLOW = 19, 20, 21
+VEL = VELOCITIES + [(0, 0, 0)] * 4
+FIELDS = range(23)
 ORDER = sorted(FIELDS, key=lambda j: (-VEL[j][0], j))
 POS = [ORDER.index(j) for j in FIELDS]
 STEPS = (-1, 0, 1)
@@ -72,9 +72,9 @@
 def row_place(g, p):
     if g < 5:
         return 2 * g + p
-    if g < 19:
+    if g < 18:
         return 10 + 14 * p + g - 5
-    return 38 + 2 * (g - 19) + p
+    return 38 + 2 * (g - 18) + p
 
 
 def messages():
@@ -98,12 +98,12 @@
 def tiles(m):
     if m[0] == "y":
         return 12 if m[1][0] == 0 else 6
-    return {"xp": 10, "xs": 8, "xa": 20, "z": 1, "l": 1}[m[0]]
+    return {"xp": 8, "xs": 8, "xa": 20, "z": 1, "l": 1}[m[0]]
 
 
 def kernel(
     sizes, dist_hbm, kinds_hbm, relax_hbm, inflow_hbm, out_ref,
-    field, kinds, block, xs, xr, ys, yr, zs, zr, ls, lr, first, second, row_tile, row_post,
+    field, kinds, either, block, xs, xr, ys, yr, zs, zr, ls, lr, first, second, row_tile, row_post,
     size_ref, load_sem, send_sem, recv_sem, entered,
 ):
     me = tuple(lax.axis_index(a) for a in AXES)
@@ -122,9 +122,10 @@
     for p in (1, 0):
         group = [
             pltpu.make_async_copy(kinds_hbm.at[p], kinds.at[p], load_sem.at[p]),
-            pltpu.make_async_copy(relax_hbm.at[p], block.at[POS[RELAX], 2 + p], load_sem.at[p]),
+            pltpu.make_async_copy(relax_hbm.at[p], either.at[0, p], load_sem.at[p]),
+            pltpu.make_async_copy(inflow_hbm.at[0, p], either.at[1, p], load_sem.at[p]),
             pltpu.make_async_copy(
-                inflow_hbm.at[:, p], block.at[POS[INFLOW] : POS[INFLOW] + 3, 2 + p], load_sem.at[p]
+                inflow_hbm.at[1:3, p], block.at[POS[INFLOW] : POS[INFLOW] + 2, 2 + p], load_sem.at[p]
             ),
             pltpu.make_async_copy(dist_hbm.at[:, p], field.at[:, p], load_sem.at[p]),
         ]
@@ -163,11 +164,11 @@
     def ends(m):
         kind, (dx, dy, dz) = m
         if kind == "xa":
-            at, mine, theirs = (slice(0, 5), slice(2, 4), slice(0, 2)) if dx == 1 else (slice(19, 24), slice(2, 4), slice(4, 6))
+            at, mine, theirs = (slice(0, 5), slice(2, 4), slice(0, 2)) if dx == 1 else (slice(18, 23), slice(2, 4), slice(4, 6))
             return block.at[at, mine], block.at[at, theirs]
         if kind == "xp":
             mine, theirs = (3, 1) if dx == 1 else (2, 4)
-            return block.at[14:19, mine : mine + 1], block.at[14:19, theirs : theirs + 1]
+            return block.at[14:18, mine : mine + 1], block.at[14:18, theirs : theirs + 1]
         if kind == "xs":
             return xs.at[side(dx)], xr.at[side(dx)]
         if kind == "y":
@@ -237,7 +238,7 @@
     def edge_lane(sign):
         return 0 if sign == 1 else 127
 
-    def collide(f, kind, relax, inflow, wanted, inside=None, level=None):
+    def collide(f, kind, own, inflow, wanted, inside=None, level=None):
         present = [i for i in range(19) if f[i] is not None]
         rho = functools.reduce(jnp.add, [f[i] for i in present])
         u = []
@@ -250,8 +251,8 @@
         wall, fluid = kind < 0.5, jnp.logical_and(kind > 0.5, kind < 1.5)
         inlet, outlet = jnp.logical_and(kind > 1.5, kind < 2.5), kind > 2.5
         r = jnp.where(outlet, one, rho)
-        v = [jnp.where(inlet, inflow[a], u[a]) for a in range(3)]
-        take = jnp.where(wall, zero, jnp.where(fluid, relax, one))
+        v = [jnp.where(inlet, given, u[a]) for a, given in enumerate((own, inflow[0], inflow[1]))]
+        take = jnp.where(wall, zero, jnp.where(fluid, own, one))
         keep = one - take
         if inside is not None:
             take, keep = take * inside, keep * inside
@@ -345,6 +346,7 @@
     for p in (1, 0):
         await_tiles(48, load_sem.at[p])
         block[POS[KIND], 2 + p] = kinds[p].astype(jnp.float32)
+        block[POS[OWN], 2 + p] = jnp.where(kinds[p] == 2, either[1, p], either[0, p])
         if p == 1:
             origin_starts([("xp", (1, 0, 0))])
         for h in (0, 1):
@@ -352,15 +354,12 @@
             post = collide(
                 [field[i, p, :, z] for i in range(19)],
                 block[POS[KIND], 2 + p, :, z],
-                block[POS[RELAX], 2 + p, :, z],
-                [block[POS[INFLOW + a], 2 + p, :, z] for a in range(3)],
+                block[POS[OWN], 2 + p, :, z],
+                [block[POS[INFLOW + a], 2 + p, :, z] for a in range(2)],
                 range(19),
             )
             for i in range(19):
                 block[POS[i], 2 + p, :, z] = post[i]
-        if p == 1:
-            sum_level(1)
-            origin_starts([("xs", (1, 0, 0))])
 
     for s in (1, -1):
         for g, (j, depth) in enumerate(ROWS[s]):
@@ -373,6 +372,17 @@
     def column(j, p, at):
         return block[POS[j], 2 + p, :, lanes(at // 128)], at % 128
 
+    tile = zero
+    for s in (1, -1):
+        for g, j in enumerate(LOCAL[s]):
+            for p in (0, 1):
+                value, at = column(j, p, 0 if s == 1 else 255)
+                to = LOCAL_LANE[s] + 4 * g + p + VEL[j][0] + 1
+                tile = jnp.where(lane_id == to, turn(value, to - at), tile)
+    ls[0] = tile
+    origin_starts([m for m in small if m[0] == "l"])
+    sum_level(1)
+    origin_starts([("xs", (1, 0, 0))])
     for s in (1, -1):
         tile = zero
         for g, (j, depth) in enumerate(COLS[s]):
@@ -381,15 +391,7 @@
                 to = 4 * g + p + VEL[j][0] + 1
                 tile = jnp.where(lane_id == to, turn(value, to - at), tile)
         zs[side(s)] = tile
-    tile = zero
-    for s in (1, -1):
-        for g, j in enumerate(LOCAL[s]):
-            for p in (0, 1):
-                value, at = column(j, p, 0 if s == 1 else 255)
-                to = LOCAL_LANE[s] + 4 * g + p + VEL[j][0] + 1
-                tile = jnp.where(lane_id == to, turn(value, to - at), tile)
-    ls[0] = tile
-    origin_starts(small + [("xa", (1, 0, 0))])
+    origin_starts([m for m in small if m[0] == "z"] + [("xa", (1, 0, 0))])
     origin_starts([m for m in rows if m[1] != (0, 1, 0)])
     sum_level(-1)
 
@@ -425,7 +427,7 @@
     await_present([m for m in MESSAGES if m[1][0] != 1], opposite, recv_sem.at[1])
 
     group_id = lane_id // 4
-    lane_cx = jnp.where(group_id < 5, -1, jnp.where(group_id < 19, 0, 1))
+    lane_cx = jnp.where(group_id < 5, -1, jnp.where(group_id < 18, 0, 1))
     lane_cx = jnp.where(group_id >= 24, jnp.where(group_id < 25, -1, jnp.where(group_id < 28, 0, 1)), lane_cx)
     source = lane_id % 4 - 1 - lane_cx
 
@@ -494,8 +496,8 @@
             post = collide(
                 [None if near and i in LEVEL else first[i, plane + 1, :, z] for i in range(19)],
                 block[POS[KIND], plane + 2, :, z],
-                block[POS[RELAX], plane + 2, :, z],
-                [block[POS[INFLOW + a], plane + 2, :, z] for a in range(3)],
+                block[POS[OWN], plane + 2, :, z],
+                [block[POS[INFLOW + a], plane + 2, :, z] for a in range(2)],
                 wanted, inside, [sums[n][h] for n in range(3)] if near else None,
             )
             for i in wanted:
@@ -553,7 +555,7 @@
     moving_y = [i for i in range(19) if VELOCITIES[i][1] != 0]
     for h in (0, 1):
         f = [row_tile[j, :, lanes(h)] for j in FIELDS]
-        post = collide(f[:19], f[KIND], f[RELAX], f[INFLOW : INFLOW + 3], moving_y, outside)
+        post = collide(f[:19], f[KIND], f[OWN], f[INFLOW : INFLOW + 2], moving_y, outside)
         for i in moving_y:
             row_post[i, :, lanes(h)] = post[i]
 
@@ -579,7 +581,7 @@
     outside = outside * jnp.where(lane_id < 8, one, beyond)
     f = [column_tile(j) for j in FIELDS]
     moving_z = [i for i in range(19) if VELOCITIES[i][2] != 0]
-    column_post = collide(f[:19], f[KIND], f[RELAX], f[INFLOW : INFLOW + 3], moving_z, outside)
+    column_post = collide(f[:19], f[KIND], f[OWN], f[INFLOW : INFLOW + 2], moving_z, outside)
 
     for p in (0, 1):
         acc = [[None, None] for _ in range(4)]
@@ -635,7 +637,8 @@
             scratch_shapes=[
                 pltpu.VMEM((19,) + shape, f32),
                 pltpu.VMEM(shape, jnp.int32),
-                pltpu.VMEM((24, 6, 8, 256), f32),
+                pltpu.VMEM((2,) + shape, f32),
+                pltpu.VMEM((23, 6, 8, 256), f32),
                 pltpu.VMEM((2, 4, 8, 256), f32),
                 pltpu.VMEM((2, 4, 8, 256), f32),
                 pltpu.VMEM((2, 48, 256), f32),
@@ -646,7 +649,7 @@
                 pltpu.VMEM((3, 3, 8, 128), f32),
                 pltpu.VMEM((19, 4, 8, 256), f32),
                 pltpu.VMEM((19, 4, 8, 256), f32),
-                pltpu.VMEM((24, 8, 256), f32),
+                pltpu.VMEM((23, 8, 256), f32),
                 pltpu.VMEM((19, 8, 256), f32),
                 pltpu.VMEM((sum(map(tiles, MESSAGES)), 8, 128), f32),
                 pltpu.SemaphoreType.DMA((2,)),

time: 19.7 us -> 19.7 us (level)
  no operation moved by 1% of the time
where the time goes in v6:
time: 19.7 us; the launch traced here: 19.5 us
  Pallas kernels  18.9 us (96%)
  between operations  0.64 us (3%)
    pallas_call x1, Pallas kernels, shards(): pl.pallas_call(functools.partial(kernel, sizes), out_shape=pltpu.VMEM((4,...  18.2 us
    pallas_call x1, Pallas kernels, shards(): pl.pallas_call(finish, out_shape=(jax.ShapeDtypeStruct(shape, f32), jax.S...  0.65 us

profile of v6, /device:TPU:65, one launch (start us, length us, event | category | flops | bytes accessed | tf_op | source)
XLA Modules:
  0.0 19.5 jit_solution(12465744992136235311)
XLA Ops:
  0.6 18.2 %shard_map.59.sums_ref = f32[4,2,8,256]{3,2,1,0:T(8,128)S(1)} custom-call(f32[19,2,8,256]{3,2,1,0:T(8,128)} %dist_hbm.1, s32[2,8,256]{2,1,0:T(8,128)} %kinds_hbm.1, f32[2,8,256]{2,1,0:T(8,128)} %relax_hbm.1, f32[3,2,8,256]{3,2,1,0:T(8,128)} %inflow_hbm.1), custom_call_target="tpu_custom_call" | custom-call | tf_op jit(solution)/shard_map/pallas_call | solution.py:632
  18.9 0.6 %shard_map.60 = (f32[2,8,256]{2,1,0:T(8,128)}, f32[3,2,8,256]{3,2,1,0:T(8,128)}) custom-call(f32[4,2,8,256]{3,2,1,0:T(8,128)S(1)} %shard_map.59.sums_ref), custom_call_target="tpu_custom_call" | custom-call | tf_op jit(solution)/shard_map/pallas_call | solution.py:662

commit v7 on v6

--- a/solution.py
+++ b/solution.py
@@ -127,7 +127,7 @@
             pltpu.make_async_copy(
                 inflow_hbm.at[1:3, p], block.at[POS[INFLOW] : POS[INFLOW] + 2, 2 + p], load_sem.at[p]
             ),
-            pltpu.make_async_copy(dist_hbm.at[:, p], field.at[:, p], load_sem.at[p]),
+            pltpu.make_async_copy(dist_hbm.at[:, p], field.at[:, p], load_sem.at[2 + p]),
         ]
         for copy in group:
             copy.start()
@@ -344,11 +344,12 @@
                     answer(d, 0)
 
     for p in (1, 0):
-        await_tiles(48, load_sem.at[p])
+        await_tiles(10, load_sem.at[p])
         block[POS[KIND], 2 + p] = kinds[p].astype(jnp.float32)
         block[POS[OWN], 2 + p] = jnp.where(kinds[p] == 2, either[1, p], either[0, p])
         if p == 1:
             origin_starts([("xp", (1, 0, 0))])
+        await_tiles(38, load_sem.at[2 + p])
         for h in (0, 1):
             z = lanes(h)
             post = collide(
@@ -360,6 +361,9 @@
             )
             for i in range(19):
                 block[POS[i], 2 + p, :, z] = post[i]
+        if p == 1:
+            sum_level(1)
+            origin_starts([("xs", (1, 0, 0))])
 
     for s in (1, -1):
         for g, (j, depth) in enumerate(ROWS[s]):
@@ -381,8 +385,6 @@
                 tile = jnp.where(lane_id == to, turn(value, to - at), tile)
     ls[0] = tile
     origin_starts([m for m in small if m[0] == "l"])
-    sum_level(1)
-    origin_starts([("xs", (1, 0, 0))])
     for s in (1, -1):
         tile = zero
         for g, (j, depth) in enumerate(COLS[s]):
@@ -652,7 +654,7 @@
                 pltpu.VMEM((23, 8, 256), f32),
                 pltpu.VMEM((19, 8, 256), f32),
                 pltpu.VMEM((sum(map(tiles, MESSAGES)), 8, 128), f32),
-                pltpu.SemaphoreType.DMA((2,)),
+                pltpu.SemaphoreType.DMA((4,)),
                 pltpu.SemaphoreType.DMA((1,)),
                 pltpu.SemaphoreType.DMA((2,)),
                 pltpu.SemaphoreType.REGULAR((2,)),

time: 19.7 us -> 19.5 us (0.990)
  Pallas kernels: 18.9 us -> 18.7 us
where the time goes in v7:
time: 19.5 us; the launch traced here: 19.3 us
  Pallas kernels  18.7 us (96%)
  between operations  0.64 us (3%)
    pallas_call x1, Pallas kernels, shards(): pl.pallas_call(functools.partial(kernel, sizes), out_shape=pltpu.VMEM((4,...  18 us
    pallas_call x1, Pallas kernels, shards(): pl.pallas_call(finish, out_shape=(jax.ShapeDtypeStruct(shape, f32), jax.S...  0.65 us

profile of v7, /device:TPU:65, one launch (start us, length us, event | category | flops | bytes accessed | tf_op | source)
XLA Modules:
  0.0 19.3 jit_solution(7856694044081248892)
XLA Ops:
  0.6 18.0 %shard_map.59.sums_ref = f32[4,2,8,256]{3,2,1,0:T(8,128)S(1)} custom-call(f32[19,2,8,256]{3,2,1,0:T(8,128)} %dist_hbm.1, s32[2,8,256]{2,1,0:T(8,128)} %kinds_hbm.1, f32[2,8,256]{2,1,0:T(8,128)} %relax_hbm.1, f32[3,2,8,256]{3,2,1,0:T(8,128)} %inflow_hbm.1), custom_call_target="tpu_custom_call" | custom-call | tf_op jit(solution)/shard_map/pallas_call | solution.py:634
  18.7 0.6 %shard_map.60 = (f32[2,8,256]{2,1,0:T(8,128)}, f32[3,2,8,256]{3,2,1,0:T(8,128)}) custom-call(f32[4,2,8,256]{3,2,1,0:T(8,128)S(1)} %shard_map.59.sums_ref), custom_call_target="tpu_custom_call" | custom-call | tf_op jit(solution)/shard_map/pallas_call | solution.py:664

commit v8 on v7

--- a/solution.py
+++ b/solution.py
@@ -82,7 +82,7 @@
     for d in DIRECTIONS:
         dx, dy, dz = d
         if dy == 0 and dz == 0:
-            found += [("xp", d), ("xs", d), ("xa", d)]
+            found += [("xp", d), ("xs", d), ("xa", d), ("xc", d)]
         if dz == 0 and dy != 0:
             found.append(("y", d))
         if dz != 0:
@@ -98,7 +98,7 @@
 def tiles(m):
     if m[0] == "y":
         return 12 if m[1][0] == 0 else 6
-    return {"xp": 8, "xs": 8, "xa": 20, "z": 1, "l": 1}[m[0]]
+    return {"xp": 8, "xs": 8, "xa": 10, "xc": 10, "z": 1, "l": 1}[m[0]]
 
 
 def kernel(
@@ -163,9 +163,11 @@
 
     def ends(m):
         kind, (dx, dy, dz) = m
-        if kind == "xa":
-            at, mine, theirs = (slice(0, 5), slice(2, 4), slice(0, 2)) if dx == 1 else (slice(18, 23), slice(2, 4), slice(4, 6))
-            return block.at[at, mine], block.at[at, theirs]
+        if kind in ("xa", "xc"):
+            at = slice(0, 5) if dx == 1 else slice(18, 23)
+            mine = 3 if (kind == "xa") == (dx == 1) else 2
+            theirs = mine - 2 * dx
+            return block.at[at, mine : mine + 1], block.at[at, theirs : theirs + 1]
         if kind == "xp":
             mine, theirs = (3, 1) if dx == 1 else (2, 4)
             return block.at[14:18, mine : mine + 1], block.at[14:18, theirs : theirs + 1]
@@ -280,7 +282,7 @@
     small = [m for m in MESSAGES if m[0] in ("z", "l")]
     small = sorted(small, key=lambda m: -sum(map(abs, m[1])))
     rows = sorted([m for m in MESSAGES if m[0] == "y"], key=lambda m: -abs(m[1][0]))
-    everything = small + [m for m in MESSAGES if m[0] in ("xp", "xs", "xa")] + rows
+    everything = small + [m for m in MESSAGES if m[0] in ("xp", "xs", "xa", "xc")] + rows
 
     def start(found):
         for m in found:
@@ -363,7 +365,7 @@
                 block[POS[i], 2 + p, :, z] = post[i]
         if p == 1:
             sum_level(1)
-            origin_starts([("xs", (1, 0, 0))])
+            origin_starts([("xs", (1, 0, 0)), ("xa", (1, 0, 0))])
 
     for s in (1, -1):
         for g, (j, depth) in enumerate(ROWS[s]):
@@ -393,7 +395,7 @@
                 to = 4 * g + p + VEL[j][0] + 1
                 tile = jnp.where(lane_id == to, turn(value, to - at), tile)
         zs[side(s)] = tile
-    origin_starts([m for m in small if m[0] == "z"] + [("xa", (1, 0, 0))])
+    origin_starts([m for m in small if m[0] == "z"] + [("xc", (1, 0, 0))])
     origin_starts([m for m in rows if m[1] != (0, 1, 0)])
     sum_level(-1)
 

time: 19.5 us -> 19.5 us (level)
  no operation moved by 1% of the time
where the time goes in v8:
time: 19.5 us; the launch traced here: 19.3 us
  Pallas kernels  18.7 us (96%)
  between operations  0.64 us (3%)
    pallas_call x1, Pallas kernels, shards(): pl.pallas_call(functools.partial(kernel, sizes), out_shape=pltpu.VMEM((4,...  18 us
    pallas_call x1, Pallas kernels, shards(): pl.pallas_call(finish, out_shape=(jax.ShapeDtypeStruct(shape, f32), jax.S...  0.65 us

profile of v8, /device:TPU:65, one launch (start us, length us, event | category | flops | bytes accessed | tf_op | source)
XLA Modules:
  0.0 19.3 jit_solution(12024793114466155383)
XLA Ops:
  0.6 18.0 %shard_map.59.sums_ref = f32[4,2,8,256]{3,2,1,0:T(8,128)S(1)} custom-call(f32[19,2,8,256]{3,2,1,0:T(8,128)} %dist_hbm.1, s32[2,8,256]{2,1,0:T(8,128)} %kinds_hbm.1, f32[2,8,256]{2,1,0:T(8,128)} %relax_hbm.1, f32[3,2,8,256]{3,2,1,0:T(8,128)} %inflow_hbm.1), custom_call_target="tpu_custom_call" | custom-call | tf_op jit(solution)/shard_map/pallas_call | solution.py:636
  18.7 0.6 %shard_map.60 = (f32[2,8,256]{2,1,0:T(8,128)}, f32[3,2,8,256]{3,2,1,0:T(8,128)}) custom-call(f32[4,2,8,256]{3,2,1,0:T(8,128)S(1)} %shard_map.59.sums_ref), custom_call_target="tpu_custom_call" | custom-call | tf_op jit(solution)/shard_map/pallas_call | solution.py:666
